TPU v7x, 256 devices: a whole 4x4x8 slice. The times are simulated.
256 devices in a mesh: section: 4 (over z_hi, core), dp: 64 (over x, y, z_lo).
Axes of the slice: x: 4, y: 4, z: 8 (z_hi: 2, z_lo: 4; z = z_hi * 4 + z_lo), core: 2. Of those that a mesh axis runs over, the one named last changes fastest.
Arguments:
- latent_states: bfloat16 [4, 256, 96, 2048], P('section', 'dp'), may hold values from -8 to 8
- rescale_factor: float32 [2048], replicated, may hold values from 0.25 to 1.75
- embedding_matrix: bfloat16 [2048, 128], P('section'), may hold values from -0.125 to 0.125
- request_span: int32 [4, 256], replicated, may hold values from 8 to 32
- passage_span: int32 [4, 256], replicated, may hold values from 32 to 64
- matching_pair: int32 [4, 256], replicated, may hold values from 0 to 255, each once within a row
- steepness_pair: float32 [2], replicated, may hold values from 8 to 400
Outputs:
- grad_hidden: bfloat16 [4, 256, 96, 2048], P('section', 'dp')
- pair_loss: float32 [4, 256], P('section', 'dp')
Inputs may be any that keep to these rules, and one draw needn't show every extreme that they name: Each matching_pair[m] names every pair of the micro-batch once.
All inputs are finite; a program needn't handle non-finite values.
Results may differ from a plain program's by a relative error of at most 0.006.
The roundings to bfloat16 on the way count: a program that leaves them out, or rounds other values in their place, can miss the bound.
Values may be sent and summed in bfloat16 or wider, within the bound.
No kernel may reach another device: no remote copies, remote signals or barrier semaphores. Data moves between devices by JAX's collectives and lax.ppermute only.
A program may use at most 64 MiB of HBM per device.

v0:
```python
import functools

import jax
import jax.numpy as jnp
from jax import lax
from jax.experimental import pallas as pl
from jax.experimental.pallas import tpu as pltpu
from jax.sharding import Mesh
from jax.sharding import PartitionSpec as P

QLEN = 32
DLEN = 64
UNROLL_F = True
UNROLL_B = True
GROUP_F = 8
GROUP_B = 8
DLEN_LEAST = 32
SECTION = ("h", "k")
PLANE = ("x", "y")
DP = ("x", "y", "z")

EPSILON = 1e-06
OBJECTIVE_FACTOR = 1024.0
MASKED = -1e30

LOG2_E = 1.4426950408889634
LN_2 = 0.6931471805599453

f32 = jnp.float32
bf16 = jnp.bfloat16


def grant(mib):
    return pltpu.CompilerParams(vmem_limit_bytes=mib * 1024 * 1024)


def vmem():
    return pl.BlockSpec(memory_space=pltpu.VMEM)


def hbm():
    return pl.BlockSpec(memory_space=pltpu.HBM)


def smem():
    return pl.BlockSpec(memory_space=pltpu.SMEM)


def rows_at(block, rows):
    start = block * rows
    return pl.ds(start if isinstance(start, int) else pl.multiple_of(start, rows), rows)


def dot_nt(a, b):
    return lax.dot_general(a, b, (((1,), (1,)), ((), ())), preferred_element_type=f32)


def dot_tn(a, b):
    return lax.dot_general(a, b, (((0,), (0,)), ((), ())), preferred_element_type=f32)


def in_turn(blocks, unroll, first, one):
    first(0, 0)

    def step(i, carry):
        first(2 * i + 1, 1)
        one(2 * i, 0)
        first(jnp.minimum(2 * i + 2, blocks - 1), 0)
        one(2 * i + 1, 1)
        return carry

    if unroll:
        for block in range(blocks):
            if block + 1 < blocks:
                first(block + 1, (block + 1) % 2)
            one(block, block % 2)
    else:
        lax.fori_loop(0, blocks // 2, step, 0)


def section_index():
    return lax.axis_index("h"), lax.axis_index("k")


def normalize_kernel(x_ref, gain_ref, normed_ref):
    values = x_ref[0].astype(f32)
    inverse_rms = lax.rsqrt(jnp.mean(values * values, axis=-1, keepdims=True) + EPSILON)
    normed_ref[0] = (values * inverse_rms * gain_ref[...]).astype(bf16)


def normalize(x, gain):
    pairs, length, width = x.shape
    rows = pl.BlockSpec((1, length, width), lambda i: (i, 0, 0))
    return pl.pallas_call(
        normalize_kernel,
        grid=(pairs,),
        in_specs=[rows, pl.BlockSpec((1, width), lambda i: (0, 0))],
        out_specs=rows,
        out_shape=jax.ShapeDtypeStruct(x.shape, bf16),
        compiler_params=grant(6),
        name="normalize",
    )(x, gain)


def project_kernel(normed_ref, own_ref, core_ref, far_ref, far_core_ref,
                   q_ref, copies_ref, proj_ref, emb_ref, d_ref, sems):
    depth = own_ref.shape[0]
    h, k = section_index()
    for ref, section in (
        (own_ref, h * 2 + k),
        (core_ref, h * 2 + 1 - k),
        (far_ref, (1 - h) * 2 + k),
        (far_core_ref, (1 - h) * 2 + 1 - k),
    ):
        emb_ref[pl.ds(pl.multiple_of(section * depth, depth), depth), :] = ref[...]
    pairs, _, _ = normed_ref.shape
    for p in range(pairs):
        projected = jnp.dot(normed_ref[p], emb_ref[...], preferred_element_type=f32)
        inverse_length = lax.rsqrt(
            jnp.sum(projected * projected, axis=-1, keepdims=True) + EPSILON
        )
        vectors = (projected * inverse_length).astype(bf16)
        q_ref[p * QLEN:(p + 1) * QLEN] = vectors[:QLEN]
        d_ref[p * DLEN:(p + 1) * DLEN] = vectors[QLEN:]
        proj_ref[p] = projected
    copies = [
        pltpu.make_async_copy(d_ref, copies_ref.at[n], sems.at[n])
        for n in range(copies_ref.shape[0])
    ]
    for copy in copies:
        copy.start()
    for copy in copies:
        copy.wait()


def project(normed, slices, readers):
    pairs, length, width = normed.shape
    _, features = slices[0].shape
    return pl.pallas_call(
        project_kernel,
        in_specs=[vmem()] * 5,
        out_specs=[vmem(), hbm(), vmem(), vmem()],
        out_shape=[
            jax.ShapeDtypeStruct((pairs * QLEN, features), bf16),
            pltpu.HBM((readers, pairs * DLEN, features), bf16),
            jax.ShapeDtypeStruct((pairs, length, features), f32),
            jax.ShapeDtypeStruct((width, features), bf16),
        ],
        scratch_shapes=[
            pltpu.VMEM((pairs * DLEN, features), bf16),
            pltpu.SemaphoreType.DMA((readers,)),
        ],
        compiler_params=grant(6),
        name="project",
    )(normed, *slices)


def ring_slot(shift, z, ring):
    return lax.rem(z + shift + ring, ring)


def place_queries(refs, all_ref):
    ring = len(refs)
    z = lax.axis_index("z")
    rows = refs[0].shape[0]
    for shift, ref in enumerate(refs):
        slot = ring_slot(-shift, z, ring)
        all_ref[pl.ds(pl.multiple_of(slot * rows, rows), rows), :] = ref[...]


def query_lanes(spans_ref, micro, first, count):
    lanes = count * QLEN
    lane = lax.broadcasted_iota(jnp.int32, (1, lanes), 1)
    owner = lax.div(lane, QLEN)
    filled = jnp.zeros((1, lanes), jnp.int32)
    for b in range(count):
        filled = jnp.where(owner == b, spans_ref[micro, first + b], filled)
    return filled


def micro_index():
    h, k = section_index()
    return h * 2 + k


def first_row():
    ring = lax.axis_size("z")
    return (lax.axis_index("x") * lax.axis_size("y") + lax.axis_index("y")) * ring


def document_pair(c, pairs):
    ring = lax.axis_size("z")
    return (lax.div(c, pairs) * ring + lax.axis_index("z")) * pairs + lax.rem(c, pairs)


def spread_sums(terms):
    _, lanes = terms.shape
    wide = 128
    same = (
        lax.div(lax.broadcasted_iota(jnp.int32, (wide, wide), 0), QLEN)
        == lax.div(lax.broadcasted_iota(jnp.int32, (wide, wide), 1), QLEN)
    ).astype(bf16)
    high = terms.astype(bf16)
    rest = terms - high.astype(f32)
    middle = rest.astype(bf16)
    low = (rest - middle.astype(f32)).astype(bf16)
    sums = []
    for at in range(0, lanes, wide):
        parts = [
            jnp.dot(part[:, at:at + wide], same, preferred_element_type=f32)
            for part in (low, middle, high)
        ]
        sums.append(parts[0] + parts[1] + parts[2])
    return jnp.concatenate(sums, axis=1)


def scores_kernel(pairs, group, request_ref, passage_ref, match_ref, steep_ref,
                  docs_ref, q0, q1, q2, q3,
                  q_all, level_ref, logits_ref, stats_ref, *sims):
    micro = micro_index()
    beta2 = steep_ref[0] * LOG2_E
    mult = steep_ref[1]
    place_queries((q0, q1, q2, q3), q_all)
    rows = group * DLEN
    blocks = docs_ref.shape[0] // rows
    lanes = q_all.shape[0]
    token = lax.broadcasted_iota(jnp.int32, (DLEN - DLEN_LEAST, 1), 0) + DLEN_LEAST

    def similarity(block, slot):
        sims[slot][...] = dot_nt(docs_ref[rows_at(block, rows), :], q_all[...])

    def pool(block, slot):
        ref = sims[slot]
        levels = []
        for n in range(group):
            c = block * group + n
            span = passage_ref[micro, document_pair(c, pairs)]
            at = n * DLEN
            early = ref[at:at + DLEN_LEAST, :]
            late = jnp.where(token < span, ref[at + DLEN_LEAST:at + DLEN, :], MASKED)
            highest = jnp.max(jnp.maximum(early, late), axis=0, keepdims=True)
            total = jnp.sum(
                jnp.exp2(beta2 * (early - highest)) + jnp.exp2(beta2 * (late - highest)),
                axis=0,
                keepdims=True,
            )
            levels.append(beta2 * highest + jnp.log2(total))
        level_ref[rows_at(block, group), :] = jnp.concatenate(levels, axis=0)

    in_turn(blocks, UNROLL_F, similarity, pool)

    count = lanes // QLEN
    first = first_row() * pairs
    span = query_lanes(request_ref, micro, first, count)
    match = query_lanes(match_ref, micro, first, count)
    lane = lax.broadcasted_iota(jnp.int32, (1, lanes), 1)
    weight = jnp.where(lax.rem(lane, QLEN) < span, 1.0, 0.0).astype(f32) / span.astype(f32)
    smooth = level_ref[...] * (LN_2 / steep_ref[0])
    logits = mult * spread_sums(smooth * weight)
    logits_ref[...] = logits
    docs = logits.shape[0]
    column = document_pair(lax.broadcasted_iota(jnp.int32, (docs, 1), 0), pairs)
    highest = jnp.max(logits, axis=0, keepdims=True)
    local = highest + jnp.log(jnp.sum(jnp.exp(logits - highest), axis=0, keepdims=True))
    positive = jnp.sum(jnp.where(column == match, logits, 0.0), axis=0, keepdims=True)
    stats_ref[...] = jnp.concatenate([local, positive], axis=0)


def scores_forward(spans, steep, docs, queries, pairs):
    rows, features = queries[0].shape
    lanes = rows * len(queries)
    count = docs.shape[0] // DLEN
    group = GROUP_F
    return pl.pallas_call(
        functools.partial(scores_kernel, pairs, group),
        in_specs=[smem()] * 4 + [vmem()] * 5,
        out_specs=[vmem()] * 4,
        out_shape=[
            jax.ShapeDtypeStruct((lanes, features), bf16),
            jax.ShapeDtypeStruct((count, lanes), f32),
            jax.ShapeDtypeStruct((count, lanes), f32),
            jax.ShapeDtypeStruct((2, lanes), f32),
        ],
        scratch_shapes=[pltpu.VMEM((group * DLEN, lanes), f32)] * 2,
        compiler_params=grant(10),
        name="scores_forward",
    )(*spans, steep, docs, *queries)


def slopes_kernel(pairs, group, request_ref, passage_ref, match_ref, steep_ref,
                  docs_ref, q_all, level_ref, logits_ref, s0, s1, s2, s3,
                  gd_ref, gq0, gq1, gq2, gq3, loss_ref,
                 sim_a, sim_b, coef_ref, gd_vmem, acc_ref, turned_ref, sem, sems):
    micro = micro_index()
    beta2 = steep_ref[0] * LOG2_E
    mult = steep_ref[1]
    rows = group * DLEN
    blocks = docs_ref.shape[0] // rows
    lanes = q_all.shape[0]
    count = lanes // QLEN
    first = first_row() * pairs
    span = query_lanes(request_ref, micro, first, count)
    match = query_lanes(match_ref, micro, first, count)
    lane = lax.broadcasted_iota(jnp.int32, (1, lanes), 1)
    weight = jnp.where(lax.rem(lane, QLEN) < span, 1.0, 0.0).astype(f32) / span.astype(f32)

    stats = [s0[...], s1[...], s2[...], s3[...]]
    locals_ = [s[0:1] for s in stats]
    highest = functools.reduce(jnp.maximum, locals_)
    total = sum(jnp.exp(l - highest) for l in locals_)
    log_total = highest + jnp.log(total)
    positive = sum(s[1:2] for s in stats)
    loss_ref[...] = log_total - positive

    docs = logits_ref.shape[0]
    column = document_pair(lax.broadcasted_iota(jnp.int32, (docs, 1), 0), pairs)
    share = jnp.exp(logits_ref[...] - log_total) - jnp.where(column == match, 1.0, 0.0)
    coef_ref[...] = weight * (OBJECTIVE_FACTOR * mult * share)

    token = lax.broadcasted_iota(jnp.int32, (DLEN - DLEN_LEAST, 1), 0) + DLEN_LEAST
    sims = (sim_a, sim_b)

    def similarity(block, slot):
        sims[slot][...] = dot_nt(docs_ref[rows_at(block, rows), :], q_all[...])

    def weigh(block, slot):
        ref = sims[slot]
        level = level_ref[rows_at(block, group), :]
        coef = coef_ref[rows_at(block, group), :]
        parts = []
        for n in range(group):
            live = passage_ref[micro, document_pair(block * group + n, pairs)]
            at = n * DLEN
            share = jnp.exp2(beta2 * ref[at:at + DLEN_LEAST, :] - level[n:n + 1])
            parts.append((coef[n:n + 1] * share).astype(bf16))
            share = jnp.exp2(beta2 * ref[at + DLEN_LEAST:at + DLEN, :] - level[n:n + 1])
            parts.append(jnp.where(token < live, coef[n:n + 1] * share, 0.0).astype(bf16))
        grad = jnp.concatenate(parts, axis=0)
        gd_vmem[rows_at(block, rows), :] = jnp.dot(
            grad, q_all[...], preferred_element_type=f32
        ).astype(gd_ref.dtype)
        acc_ref[...] += dot_tn(docs_ref[rows_at(block, rows), :], grad)

    acc_ref[...] = jnp.zeros_like(acc_ref)
    in_turn(blocks, UNROLL_B, similarity, weigh)
    out = pltpu.make_async_copy(gd_vmem.reshape(gd_ref.shape), gd_ref, sem)
    out.start()
    parts = (gq0, gq1, gq2, gq3)
    own = lanes // len(parts)
    turned_ref[...] = acc_ref[...].T
    z = lax.axis_index("z")
    sends = [out]
    for shift, ref in enumerate(parts):
        at = rows_at(ring_slot(shift, z, len(parts)), own)
        sends.append(pltpu.make_async_copy(turned_ref.at[at], ref, sems.at[shift]))
        sends[-1].start()
    for send in sends:
        send.wait()


def slopes(spans, steep, docs, q_all, level, logits, stats, pairs, block_shape):
    lanes, features = q_all.shape
    count = level.shape[0]
    group = GROUP_B
    return pl.pallas_call(
        functools.partial(slopes_kernel, pairs, group),
        in_specs=[smem()] * 4 + [vmem()] * 8,
        out_specs=[hbm()] * (len(stats) + 1) + [vmem()],
        out_shape=[
            pltpu.HBM(block_shape, bf16),
            *[pltpu.HBM((lanes // len(stats), features), f32)] * len(stats),
            jax.ShapeDtypeStruct((1, lanes), f32),
        ],
        scratch_shapes=[
            pltpu.VMEM((group * DLEN, lanes), f32),
            pltpu.VMEM((group * DLEN, lanes), f32),
            pltpu.VMEM((count, lanes), f32),
            pltpu.VMEM(docs.shape, bf16),
            pltpu.VMEM((features, lanes), f32),
            pltpu.VMEM((lanes, features), f32),
            pltpu.SemaphoreType.DMA,
            pltpu.SemaphoreType.DMA((len(stats),)),
        ],
        compiler_params=grant(16),
        name="slopes",
    )(*spans, steep, docs, q_all, level, logits, *stats)


def head_backward_kernel(x_ref, gain_ref, emb_ref, proj_ref, gd_ref, g0, g1, g2, g3, out_ref,
                         out_vmem, sems):
    pairs = x_ref.shape[0]
    sends = []
    for p in range(pairs):
        at = slice(p * QLEN, (p + 1) * QLEN)
        grad_query = g0[at] + g1[at] + g2[at] + g3[at]
        grad_docs = jnp.sum(gd_ref[:, p * DLEN:(p + 1) * DLEN].astype(f32), axis=0)
        grad_vectors = jnp.concatenate([grad_query, grad_docs], axis=0)
        projected = proj_ref[p]
        inverse_length = lax.rsqrt(
            jnp.sum(projected * projected, axis=-1, keepdims=True) + EPSILON
        )
        unit = projected * inverse_length
        along = jnp.sum(unit * grad_vectors, axis=-1, keepdims=True)
        grad_projected = (inverse_length * (grad_vectors - unit * along)).astype(bf16)
        values = x_ref[p].astype(f32)
        inverse_rms = lax.rsqrt(jnp.mean(values * values, axis=-1, keepdims=True) + EPSILON)
        weighted = dot_nt(grad_projected, emb_ref[...]) * gain_ref[...]
        mean_term = jnp.mean(values * weighted, axis=-1, keepdims=True)
        out_vmem[p] = (
            inverse_rms * weighted
            - values * (inverse_rms * inverse_rms * inverse_rms) * mean_term
        ).astype(bf16)
        sends.append(pltpu.make_async_copy(out_vmem.at[p], out_ref.at[p], sems.at[p]))
        sends[-1].start()
    for send in sends:
        send.wait()


def head_backward(x, gain, emb, projected, grad_docs, grad_queries):
    pairs = x.shape[0]
    return pl.pallas_call(
        head_backward_kernel,
        in_specs=[vmem()] * 9,
        out_specs=hbm(),
        out_shape=jax.ShapeDtypeStruct(x.shape, bf16),
        scratch_shapes=[pltpu.VMEM(x.shape, bf16), pltpu.SemaphoreType.DMA((pairs,))],
        compiler_params=grant(10),
        name="head_backward",
    )(x, gain, emb, projected, grad_docs, *grad_queries)


def all_slices(own):
    swap = [(0, 1), (1, 0)]
    ring = lax.axis_size("z")
    mirror = [
        (h * ring + z, (1 - h) * ring + ring - 1 - z) for h in range(2) for z in range(ring)
    ]
    far = lax.ppermute(own, ("h", "z"), mirror)
    core = lax.ppermute(own, "k", swap)
    far_core = lax.ppermute(far, "k", swap)
    return own, core, far, far_core


def turned(array, shift):
    ring = lax.axis_size("z")
    return lax.ppermute(array, "z", [(i, (i + shift) % ring) for i in range(ring)])


def local(x, gain, embedding, request_span, passage_span, matching_pair, steepness):
    x = x[0]
    pairs = x.shape[0]
    ring = lax.axis_size("z")
    gain = gain[None]
    spans = (request_span, passage_span, matching_pair)
    plane = lax.axis_size(PLANE)
    normed = normalize(x, gain)
    slices = all_slices(embedding)
    q, copies, projected, emb = project(normed, slices, plane)
    queries = [q] + [turned(q, s) for s in range(1, ring)]
    docs = lax.all_to_all(copies, PLANE, split_axis=0, concat_axis=0, tiled=True)
    docs = docs.reshape(-1, docs.shape[-1])
    q_all, level, logits, stats = scores_forward(spans, steepness, docs, queries, pairs)
    stats = [stats] + [turned(stats, s) for s in range(1, ring)]
    gd, *parts, loss = slopes(
        spans, steepness, docs, q_all, level, logits, stats, pairs, copies.shape
    )
    grad_docs = lax.all_to_all(gd, PLANE, split_axis=0, concat_axis=0, tiled=True)
    grad_queries = [parts[0]] + [turned(parts[s], s) for s in range(1, ring)]
    grad_x = head_backward(x, gain, emb, projected, grad_docs, grad_queries)
    own = lax.dynamic_slice_in_dim(
        loss.reshape(ring, pairs, QLEN)[:, :, 0], lax.axis_index("z"), 1, 0
    )
    return grad_x[None], own


def solution(mesh):
    side = round(mesh.shape["dp"] ** (1 / 3))
    finer = Mesh(mesh.devices.reshape(2, 2, side, side, side), ("h", "k", "x", "y", "z"))
    rows = P(SECTION, DP, None, None)
    return jax.shard_map(
        local,
        mesh=finer,
        in_specs=(rows, P(), P(SECTION, None), P(), P(), P(), P()),
        out_specs=(rows, P(SECTION, DP)),
        check_vma=False,
    )
```

profile of v0, /device:TPU:8, one launch (start us, length us, event | category | flops | bytes accessed | tf_op | source)
XLA Modules:
  0.0 79.7 jit_solution(8481213159324921043)
XLA Ops:
  0.6 5.9 %collective-permute-start.1 = (bf16[512,128]{1,0:T(8,128)(2,1)}, bf16[512,128]{1,0:T(8,128)(2,1)S(1)}, u32[]{:S(2)}, u32[]{:S(2)}) collective-permute-start(bf16[512,128]{1,0:T(8,128)(2,1)} %own_ref.1), channel_id=1, source_target_pairs={{0,131},{1,130},{2,129},{3,128},{128,3},{129,2},{130,1},{131,0},{4... | collective-permute-start | bytes 393224 | tf_op jit(solution)/shard_map/ppermute | solution.py:438
  6.6 0.0 collective-permute-start
  6.6 6.5 %collective-permute-done.1.far_ref = bf16[512,128]{1,0:T(8,128)(2,1)S(1)} collective-permute-done((bf16[512,128]{1,0:T(8,128)(2,1)}, bf16[512,128]{1,0:T(8,128)(2,1)S(1)}, u32[]{:S(2)}, u32[]{:S(2)}) %collective-permute-start.1) | collective-permute-done | bytes 131104 | tf_op jit(solution)/shard_map/ppermute | solution.py:438
  13.1 0.0 collective-permute-start.2
  13.1 1.4 %copy-done = bf16[1,4,96,2048]{3,2,1,0:T(8,128)(2,1)S(1)} copy-done((bf16[1,4,96,2048]{3,2,1,0:T(8,128)(2,1)S(1)}, bf16[1,4,96,2048]{3,2,1,0:T(8,128)(2,1)}, u32[]{:S(2)}) %copy-start) | copy-done | bytes 1572888
  14.5 0.7 copy-done.4
  15.2 0.8 normalize.1.normed_ref
  16.0 0.0 collective-permute-done.core_ref
  16.0 0.0 collective-permute-done.2.far_core_ref
  16.0 0.1 copy-done.2
  16.1 1.8 %project.1 = (bf16[128,128]{1,0:T(8,128)(2,1)S(1)}, bf16[16,256,128]{2,1,0:T(8,128)(2,1)}, f32[4,96,128]{2,1,0:T(8,128)S(1)}, bf16[2048,128]{1,0:T(8,128)(2,1)S(1)}) custom-call(bf16[4,96,2048]{2,1,0:T(8,128)(2,1)S(1)} %normalize.1.normed_ref, bf16[512,128]{1,0:T(8,128)(2,1)S(1)} %copy-done.2, bf16[512,128]{1,0:T(8,128)(2,1)S(1)} %collective-permute-done.core_ref, ...), custom_call_target="tpu_custom_call" | custom-call | tf_op jit(solution)/shard_map/project/pallas_call | solution.py:139
  17.9 0.0 copy-start.6
  17.9 0.0 copy-start.7
  17.9 0.0 copy-start.8
  17.9 0.0 copy-start.9
  18.0 7.5 %all-to-all-start = ((bf16[16,256,128]{2,1,0:T(8,128)(2,1)}), bf16[16,256,128]{2,1,0:T(8,128)(2,1)S(1)}, u32[]{:S(2)}, u32[]{:S(2)}) async-start(bf16[16,256,128]{2,1,0:T(8,128)(2,1)} %get-tuple-element.18), calls=%async_computation | async-start | bytes 2097152 | tf_op jit(solution)/shard_map/all_to_all | solution.py:460
  25.5 0.0 collective-permute-start.3
  25.5 2.4 %collective-permute-start.4 = (bf16[128,128]{1,0:T(8,128)(2,1)S(1)}, bf16[128,128]{1,0:T(8,128)(2,1)S(1)}, u32[]{:S(2)}, u32[]{:S(2)}) collective-permute-start(bf16[128,128]{1,0:T(8,128)(2,1)S(1)} %get-tuple-element.19.q0), channel_id=1, source_target_pairs={{0,2},{1,3},{2,0},{3,1},{4,6},{5,7},{6,4},{7,5},{8,10},{9,11},{10,... | collective-permute-start | bytes 98312 | tf_op jit(solution)/shard_map/ppermute | solution.py:446
  27.9 1.4 %collective-permute-start.5 = (bf16[128,128]{1,0:T(8,128)(2,1)S(1)}, bf16[128,128]{1,0:T(8,128)(2,1)S(1)}, u32[]{:S(2)}, u32[]{:S(2)}) collective-permute-start(bf16[128,128]{1,0:T(8,128)(2,1)S(1)} %get-tuple-element.19.q0), channel_id=1, source_target_pairs={{0,3},{1,0},{2,1},{3,2},{4,7},{5,4},{6,5},{7,6},{8,11},{9,8},{10,9... | collective-permute-start | bytes 98312 | tf_op jit(solution)/shard_map/ppermute | solution.py:446
  29.3 1.9 %collective-permute-done.3.q1 = bf16[128,128]{1,0:T(8,128)(2,1)S(1)} collective-permute-done((bf16[128,128]{1,0:T(8,128)(2,1)S(1)}, bf16[128,128]{1,0:T(8,128)(2,1)S(1)}, u32[]{:S(2)}, u32[]{:S(2)}) %collective-permute-start.3) | collective-permute-done | bytes 32800 | tf_op jit(solution)/shard_map/ppermute | solution.py:446
  31.2 0.0 collective-permute-done.4.q2
  31.2 0.6 collective-permute-done.5.q3
  31.9 10.7 %all-to-all-done = bf16[16,256,128]{2,1,0:T(8,128)(2,1)S(1)} async-done(((bf16[16,256,128]{2,1,0:T(8,128)(2,1)}), bf16[16,256,128]{2,1,0:T(8,128)(2,1)S(1)}, u32[]{:S(2)}, u32[]{:S(2)}) %all-to-all-start) | async-done | bytes 1048608 | tf_op jit(solution)/shard_map/all_to_all | solution.py:460
  42.6 0.0 copy-done.6
  42.6 0.0 copy-done.8
  42.6 3.8 %scores_forward.1 = (bf16[512,128]{1,0:T(8,128)(2,1)S(1)}, f32[64,512]{1,0:T(8,128)S(1)}, f32[64,512]{1,0:T(8,128)S(1)}, f32[2,512]{1,0:T(2,128)S(1)}) custom-call(s32[4,256]{1,0:T(4,128)S(1)} %copy-done.6, s32[4,256]{1,0:T(4,128)S(1)} %copy-done.7, s32[4,256]{1,0:T(4,128)S(1)} %copy-done.8, f32[2]{0:T(128)S(1)} %copy-done.9, bf16[4096,128]{1,0:T(8,128)(2,1)S(1)} %bitcast.6, ...), custom_call_target="tpu_custom_call" | custom-call | tf_op jit(solution)/shard_map/scores_forward/pallas_call | solution.py:274
  46.4 0.1 collective-permute-start.6
  46.5 2.4 %collective-permute-start.7 = (f32[2,512]{1,0:T(2,128)S(1)}, f32[2,512]{1,0:T(2,128)S(1)}, u32[]{:S(2)}, u32[]{:S(2)}) collective-permute-start(f32[2,512]{1,0:T(2,128)S(1)} %get-tuple-element.23.s0), channel_id=1, source_target_pairs={{0,2},{1,3},{2,0},{3,1},{4,6},{5,7},{6,4},{7,5},{8,10},{9,11},{10,... | collective-permute-start | bytes 12296 | tf_op jit(solution)/shard_map/ppermute | solution.py:446
  49.0 1.4 %collective-permute-start.8 = (f32[2,512]{1,0:T(2,128)S(1)}, f32[2,512]{1,0:T(2,128)S(1)}, u32[]{:S(2)}, u32[]{:S(2)}) collective-permute-start(f32[2,512]{1,0:T(2,128)S(1)} %get-tuple-element.23.s0), channel_id=1, source_target_pairs={{0,3},{1,0},{2,1},{3,2},{4,7},{5,4},{6,5},{7,6},{8,11},{9,8},{10,9... | collective-permute-start | bytes 12296 | tf_op jit(solution)/shard_map/ppermute | solution.py:446
  50.3 1.6 %collective-permute-done.6.s1 = f32[2,512]{1,0:T(2,128)S(1)} collective-permute-done((f32[2,512]{1,0:T(2,128)S(1)}, f32[2,512]{1,0:T(2,128)S(1)}, u32[]{:S(2)}, u32[]{:S(2)}) %collective-permute-start.6) | collective-permute-done | bytes 4128 | tf_op jit(solution)/shard_map/ppermute | solution.py:446
  51.9 0.0 collective-permute-done.7.s2
  51.9 0.7 collective-permute-done.8.s3
  52.6 4.8 %slopes.1 = (bf16[16,256,128]{2,1,0:T(8,128)(2,1)}, f32[128,128]{1,0:T(8,128)}, f32[128,128]{1,0:T(8,128)}, f32[128,128]{1,0:T(8,128)}, f32[128,128]{1,0:T(8,128)}, /*index=5*/f32[1,512]{1,0:T(1,128)S(1)}) custom-call(s32[4,256]{1,0:T(4,128)S(1)} %copy-done.6, s32[4,256]{1,0:T(4,128)S(1)} %copy-done.7, s32[4,256]{1,0:T(4,128)S(1)} %copy-done.8, ...), custom_call_target="tpu_custom_call" | custom-call | tf_op jit(solution)/shard_map/slopes/pallas_call | solution.py:365
  57.4 5.1 %all-to-all-start.1 = ((bf16[16,256,128]{2,1,0:T(8,128)(2,1)}), bf16[16,256,128]{2,1,0:T(8,128)(2,1)S(1)}, u32[]{:S(2)}, u32[]{:S(2)}) async-start(bf16[16,256,128]{2,1,0:T(8,128)(2,1)} %get-tuple-element.24), calls=%async_computation.1 | async-start | bytes 2097152 | tf_op jit(solution)/shard_map/all_to_all | solution.py:467
  62.5 1.1 %collective-permute-start.10 = (f32[128,128]{1,0:T(8,128)}, f32[128,128]{1,0:T(8,128)S(1)}, u32[]{:S(2)}, u32[]{:S(2)}) collective-permute-start(f32[128,128]{1,0:T(8,128)} %get-tuple-element.27), channel_id=1, source_target_pairs={{0,2},{1,3},{2,0},{3,1},{4,6},{5,7},{6,4},{7,5},{8,10},{9,11},{10,... | collective-permute-start | bytes 196616 | tf_op jit(solution)/shard_map/ppermute | solution.py:446
  63.6 3.2 %collective-permute-start.11 = (f32[128,128]{1,0:T(8,128)}, f32[128,128]{1,0:T(8,128)S(1)}, u32[]{:S(2)}, u32[]{:S(2)}) collective-permute-start(f32[128,128]{1,0:T(8,128)} %get-tuple-element.28), channel_id=1, source_target_pairs={{0,3},{1,0},{2,1},{3,2},{4,7},{5,4},{6,5},{7,6},{8,11},{9,8},{10,9... | collective-permute-start | bytes 196616 | tf_op jit(solution)/shard_map/ppermute | solution.py:446
  66.8 0.0 collective-permute-start.9
  66.8 0.5 broadcast.3
  67.3 0.7 reduce.3
  67.9 0.7 reshape.12
  68.6 0.7 constant_dynamic-slice_fusion
  69.3 0.6 copy.11
  69.9 0.0 collective-permute-done.10.g2
  69.9 0.0 collective-permute-done.11.g3
  69.9 3.2 %collective-permute-done.9.g1 = f32[128,128]{1,0:T(8,128)} collective-permute-done((f32[128,128]{1,0:T(8,128)}, f32[128,128]{1,0:T(8,128)}, u32[]{:S(2)}, u32[]{:S(2)}) %collective-permute-start.9) | collective-permute-done | bytes 65568 | tf_op jit(solution)/shard_map/ppermute | solution.py:446
  73.1 3.0 %all-to-all-done.1.gd_ref = bf16[16,256,128]{2,1,0:T(8,128)(2,1)S(1)} async-done(((bf16[16,256,128]{2,1,0:T(8,128)(2,1)}), bf16[16,256,128]{2,1,0:T(8,128)(2,1)S(1)}, u32[]{:S(2)}, u32[]{:S(2)}) %all-to-all-start.1) | async-done | bytes 1048608 | tf_op jit(solution)/shard_map/all_to_all | solution.py:467
  76.1 0.0 copy-done.5
  76.1 3.4 %head_backward.1 = bf16[4,96,2048]{2,1,0:T(8,128)(2,1)} custom-call(bf16[4,96,2048]{2,1,0:T(8,128)(2,1)S(1)} %bitcast.9, f32[1,2048]{1,0:T(1,128)S(1)} %bitcast.11, bf16[2048,128]{1,0:T(8,128)(2,1)S(1)} %get-tuple-element.16.emb_ref, f32[4,96,128]{2,1,0:T(8,128)S(1)} %get-tuple-element.17.proj_ref, bf16[16,256,128]{2,1,0:T(8,128)(2,1)S(1)} %all-to-all-done.1.gd_ref, ...), custom_call_target="tpu_custom_call" | custom-call | tf_op jit(solution)/shard_map/head_backward/pallas_call | solution.py:421
  (10 shorter events, 0.0 us)
Async XLA Ops:
  0.6 12.5 %collective-permute-start.1 = (bf16[512,128]{1,0:T(8,128)(2,1)}, bf16[512,128]{1,0:T(8,128)(2,1)S(1)}, u32[]{:S(2)}, u32[]{:S(2)}) collective-permute-start(bf16[512,128]{1,0:T(8,128)(2,1)} %own_ref.1), channel_id=1, source_target_pairs={{0,131},{1,130},{2,129},{3,128},{128,3},{129,2},{130,1},{131,0},{4... | collective-permute-start | bytes 393224 | tf_op jit(solution)/shard_map/ppermute | solution.py:438
  6.6 9.4 %collective-permute-start = (bf16[512,128]{1,0:T(8,128)(2,1)}, bf16[512,128]{1,0:T(8,128)(2,1)S(1)}, u32[]{:S(2)}, u32[]{:S(2)}) collective-permute-start(bf16[512,128]{1,0:T(8,128)(2,1)} %own_ref.1), channel_id=1, source_target_pairs={{0,64},{64,0},{1,65},{65,1},{2,66},{66,2},{3,67},{67,3},{4,68},{68... | collective-permute-start | bytes 393224 | tf_op jit(solution)/shard_map/ppermute | solution.py:439
  13.1 2.9 %collective-permute-start.2 = (bf16[512,128]{1,0:T(8,128)(2,1)S(1)}, bf16[512,128]{1,0:T(8,128)(2,1)S(1)}, u32[]{:S(2)}, u32[]{:S(2)}) collective-permute-start(bf16[512,128]{1,0:T(8,128)(2,1)S(1)} %collective-permute-done.1.far_ref), channel_id=1, source_target_pairs={{0,64},{64,0},{1,65},{65,1},{2,66},{66,2},{3,67},{67,3},{4,68},{68... | collective-permute-start | bytes 393224 | tf_op jit(solution)/shard_map/ppermute | solution.py:440
  13.1 1.4 %copy-start = (bf16[1,4,96,2048]{3,2,1,0:T(8,128)(2,1)S(1)}, bf16[1,4,96,2048]{3,2,1,0:T(8,128)(2,1)}, u32[]{:S(2)}) copy-start(bf16[1,4,96,2048]{3,2,1,0:T(8,128)(2,1)} %param.7) | copy-start | bytes 4718596
  14.5 0.7 copy-start.4
  15.2 0.9 %copy-start.2 = (bf16[512,128]{1,0:T(8,128)(2,1)S(1)}, bf16[512,128]{1,0:T(8,128)(2,1)}, u32[]{:S(2)}) copy-start(bf16[512,128]{1,0:T(8,128)(2,1)} %own_ref.1) | copy-start | bytes 393220
  17.9 24.7 %copy-start.6 = (s32[4,256]{1,0:T(4,128)S(1)}, s32[4,256]{1,0:T(4,128)}, u32[]{:S(2)}) copy-start(s32[4,256]{1,0:T(4,128)} %request_ref.3) | copy-start | bytes 12292
  17.9 24.7 %copy-start.7 = (s32[4,256]{1,0:T(4,128)S(1)}, s32[4,256]{1,0:T(4,128)}, u32[]{:S(2)}) copy-start(s32[4,256]{1,0:T(4,128)} %passage_ref.3) | copy-start | bytes 12292
  17.9 24.7 %copy-start.8 = (s32[4,256]{1,0:T(4,128)S(1)}, s32[4,256]{1,0:T(4,128)}, u32[]{:S(2)}) copy-start(s32[4,256]{1,0:T(4,128)} %match_ref.3) | copy-start | bytes 12292
  17.9 24.7 %copy-start.9 = (f32[2]{0:T(128)S(1)}, f32[2]{0:T(128)}, u32[]{:S(2)}) copy-start(f32[2]{0:T(128)} %steep_ref.3) | copy-start | bytes 28
  18.0 24.6 %all-to-all-start = ((bf16[16,256,128]{2,1,0:T(8,128)(2,1)}), bf16[16,256,128]{2,1,0:T(8,128)(2,1)S(1)}, u32[]{:S(2)}, u32[]{:S(2)}) async-start(bf16[16,256,128]{2,1,0:T(8,128)(2,1)} %get-tuple-element.18), calls=%async_computation | async-start | bytes 2097152 | tf_op jit(solution)/shard_map/all_to_all | solution.py:460
  25.5 5.7 %collective-permute-start.3 = (bf16[128,128]{1,0:T(8,128)(2,1)S(1)}, bf16[128,128]{1,0:T(8,128)(2,1)S(1)}, u32[]{:S(2)}, u32[]{:S(2)}) collective-permute-start(bf16[128,128]{1,0:T(8,128)(2,1)S(1)} %get-tuple-element.19.q0), channel_id=1, source_target_pairs={{0,1},{1,2},{2,3},{3,0},{4,5},{5,6},{6,7},{7,4},{8,9},{9,10},{10,1... | collective-permute-start | bytes 98312 | tf_op jit(solution)/shard_map/ppermute | solution.py:446
  25.5 5.7 %collective-permute-start.4 = (bf16[128,128]{1,0:T(8,128)(2,1)S(1)}, bf16[128,128]{1,0:T(8,128)(2,1)S(1)}, u32[]{:S(2)}, u32[]{:S(2)}) collective-permute-start(bf16[128,128]{1,0:T(8,128)(2,1)S(1)} %get-tuple-element.19.q0), channel_id=1, source_target_pairs={{0,2},{1,3},{2,0},{3,1},{4,6},{5,7},{6,4},{7,5},{8,10},{9,11},{10,... | collective-permute-start | bytes 98312 | tf_op jit(solution)/shard_map/ppermute | solution.py:446
  27.9 3.9 %collective-permute-start.5 = (bf16[128,128]{1,0:T(8,128)(2,1)S(1)}, bf16[128,128]{1,0:T(8,128)(2,1)S(1)}, u32[]{:S(2)}, u32[]{:S(2)}) collective-permute-start(bf16[128,128]{1,0:T(8,128)(2,1)S(1)} %get-tuple-element.19.q0), channel_id=1, source_target_pairs={{0,3},{1,0},{2,1},{3,2},{4,7},{5,4},{6,5},{7,6},{8,11},{9,8},{10,9... | collective-permute-start | bytes 98312 | tf_op jit(solution)/shard_map/ppermute | solution.py:446
  46.4 5.5 %collective-permute-start.6 = (f32[2,512]{1,0:T(2,128)S(1)}, f32[2,512]{1,0:T(2,128)S(1)}, u32[]{:S(2)}, u32[]{:S(2)}) collective-permute-start(f32[2,512]{1,0:T(2,128)S(1)} %get-tuple-element.23.s0), channel_id=1, source_target_pairs={{0,1},{1,2},{2,3},{3,0},{4,5},{5,6},{6,7},{7,4},{8,9},{9,10},{10,1... | collective-permute-start | bytes 12296 | tf_op jit(solution)/shard_map/ppermute | solution.py:446
  46.5 5.4 %collective-permute-start.7 = (f32[2,512]{1,0:T(2,128)S(1)}, f32[2,512]{1,0:T(2,128)S(1)}, u32[]{:S(2)}, u32[]{:S(2)}) collective-permute-start(f32[2,512]{1,0:T(2,128)S(1)} %get-tuple-element.23.s0), channel_id=1, source_target_pairs={{0,2},{1,3},{2,0},{3,1},{4,6},{5,7},{6,4},{7,5},{8,10},{9,11},{10,... | collective-permute-start | bytes 12296 | tf_op jit(solution)/shard_map/ppermute | solution.py:446
  49.0 3.6 %collective-permute-start.8 = (f32[2,512]{1,0:T(2,128)S(1)}, f32[2,512]{1,0:T(2,128)S(1)}, u32[]{:S(2)}, u32[]{:S(2)}) collective-permute-start(f32[2,512]{1,0:T(2,128)S(1)} %get-tuple-element.23.s0), channel_id=1, source_target_pairs={{0,3},{1,0},{2,1},{3,2},{4,7},{5,4},{6,5},{7,6},{8,11},{9,8},{10,9... | collective-permute-start | bytes 12296 | tf_op jit(solution)/shard_map/ppermute | solution.py:446
  52.6 23.5 %copy-start.1 = (bf16[1,4,96,2048]{3,2,1,0:T(8,128)(2,1)S(1)}, bf16[1,4,96,2048]{3,2,1,0:T(8,128)(2,1)}, u32[]{:S(2)}) copy-start(bf16[1,4,96,2048]{3,2,1,0:T(8,128)(2,1)} %param.7) | copy-start | bytes 4718596
  52.6 23.5 %copy-start.5 = (f32[2048]{0:T(1024)S(1)}, f32[2048]{0:T(1024)}, u32[]{:S(2)}) copy-start(f32[2048]{0:T(1024)} %param.8) | copy-start | bytes 24580
  57.4 18.7 %copy-start.3 = (f32[128,128]{1,0:T(8,128)S(1)}, f32[128,128]{1,0:T(8,128)}, u32[]{:S(2)}) copy-start(f32[128,128]{1,0:T(8,128)} %get-tuple-element.25.g0) | copy-start | bytes 196612
  57.4 18.7 %all-to-all-start.1 = ((bf16[16,256,128]{2,1,0:T(8,128)(2,1)}), bf16[16,256,128]{2,1,0:T(8,128)(2,1)S(1)}, u32[]{:S(2)}, u32[]{:S(2)}) async-start(bf16[16,256,128]{2,1,0:T(8,128)(2,1)} %get-tuple-element.24), calls=%async_computation.1 | async-start | bytes 2097152 | tf_op jit(solution)/shard_map/all_to_all | solution.py:467
  62.5 7.4 %collective-permute-start.10 = (f32[128,128]{1,0:T(8,128)}, f32[128,128]{1,0:T(8,128)S(1)}, u32[]{:S(2)}, u32[]{:S(2)}) collective-permute-start(f32[128,128]{1,0:T(8,128)} %get-tuple-element.27), channel_id=1, source_target_pairs={{0,2},{1,3},{2,0},{3,1},{4,6},{5,7},{6,4},{7,5},{8,10},{9,11},{10,... | collective-permute-start | bytes 196616 | tf_op jit(solution)/shard_map/ppermute | solution.py:446
  63.6 6.3 %collective-permute-start.11 = (f32[128,128]{1,0:T(8,128)}, f32[128,128]{1,0:T(8,128)S(1)}, u32[]{:S(2)}, u32[]{:S(2)}) collective-permute-start(f32[128,128]{1,0:T(8,128)} %get-tuple-element.28), channel_id=1, source_target_pairs={{0,3},{1,0},{2,1},{3,2},{4,7},{5,4},{6,5},{7,6},{8,11},{9,8},{10,9... | collective-permute-start | bytes 196616 | tf_op jit(solution)/shard_map/ppermute | solution.py:446
  66.8 6.4 %collective-permute-start.9 = (f32[128,128]{1,0:T(8,128)}, f32[128,128]{1,0:T(8,128)}, u32[]{:S(2)}, u32[]{:S(2)}) collective-permute-start(f32[128,128]{1,0:T(8,128)} %get-tuple-element.26), channel_id=1, source_target_pairs={{0,1},{1,2},{2,3},{3,0},{4,5},{5,6},{6,7},{7,4},{8,9},{9,10},{10,1... | collective-permute-start | bytes 196616 | tf_op jit(solution)/shard_map/ppermute | solution.py:446
where the time goes:
time: 80.9 us; the launch traced here: 79.7 us
  starting transfers between devices  30.6 us (38%)
  waiting for transfers between devices  28.2 us (35%)
  Pallas kernels  14.6 us (18%)
  local copies, waits for them, and re-layouts  4.7 us (6%)
  between operations  0.92 us (1%)
    ppermute x9, starting transfers between devices, turned(): lax.ppermute(array, 'z', [(i, (i + shift) % ring) for i in range(ring)])  12 us
    all_to_all x1, waiting for transfers between devices, local(): lax.all_to_all(copies, PLANE, split_axis=0, concat_axis=0, tiled=True)  10.7 us
    ppermute x9, waiting for transfers between devices, turned(): lax.ppermute(array, 'z', [(i, (i + shift) % ring) for i in range(ring)])  8.02 us
    all_to_all x1, starting transfers between devices, local(): lax.all_to_all(copies, PLANE, split_axis=0, concat_axis=0, tiled=True)  7.53 us
    ppermute x1, waiting for transfers between devices, all_slices(): far = lax.ppermute(own, ('h', 'z'), mirror)  6.51 us
    ppermute x1, starting transfers between devices, all_slices(): far = lax.ppermute(own, ('h', 'z'), mirror)  5.94 us
    all_to_all x1, starting transfers between devices, local(): lax.all_to_all(gd, PLANE, split_axis=0, concat_axis=0, tiled=True)  5.06 us
    pallas_call x1, Pallas kernels, slopes(): pl.pallas_call(functools.partial(slopes_kernel, pairs, group), in_specs=[...  4.8 us
  transfers between devices with their start and end apart: 14, of which 8 were waited for; matrix products, arithmetic and copies ran while one was open for 4% of the time, Pallas kernels for 1%

commit v1 on v0

v1 whole, which is shorter than its diff:
```python
import functools

import jax
import jax.numpy as jnp
from jax import lax
from jax.experimental import pallas as pl
from jax.experimental.pallas import tpu as pltpu
from jax.sharding import Mesh
from jax.sharding import PartitionSpec as P

QLEN = 32
DLEN = 64
LANES = 128
GROUP = 8
CHUNK = 512
DLEN_LEAST = 32
SECTION = ("h", "k")
PLANE = ("x", "y")
DP = ("x", "y", "z")

EPSILON = 1e-06
OBJECTIVE_FACTOR = 1024.0
MASKED = -1e30

LOG2_E = 1.4426950408889634
LN_2 = 0.6931471805599453

f32 = jnp.float32
bf16 = jnp.bfloat16


def grant(mib):
    return pltpu.CompilerParams(vmem_limit_bytes=mib * 1024 * 1024)


def vmem():
    return pl.BlockSpec(memory_space=pltpu.VMEM)


def hbm():
    return pl.BlockSpec(memory_space=pltpu.HBM)


def smem():
    return pl.BlockSpec(memory_space=pltpu.SMEM)


def dot_nt(a, b):
    return lax.dot_general(a, b, (((1,), (1,)), ((), ())), preferred_element_type=f32)


def dot_tn(a, b):
    return lax.dot_general(a, b, (((0,), (0,)), ((), ())), preferred_element_type=f32)


def in_turn(blocks, fill, use):
    fill(0, 0)
    for block in range(blocks):
        if block + 1 < blocks:
            fill(block + 1, (block + 1) % 2)
        use(block, block % 2)


def section_index():
    return lax.axis_index("h"), lax.axis_index("k")


def normalize_kernel(x_ref, gain_ref, normed_ref):
    values = x_ref[0].astype(f32)
    inverse_rms = lax.rsqrt(jnp.mean(values * values, axis=-1, keepdims=True) + EPSILON)
    normed_ref[0] = (values * inverse_rms * gain_ref[...]).astype(bf16)


def normalize(x, gain):
    pairs, length, width = x.shape
    rows = pl.BlockSpec((1, length, width), lambda i: (i, 0, 0))
    return pl.pallas_call(
        normalize_kernel,
        grid=(pairs,),
        in_specs=[rows, pl.BlockSpec((1, width), lambda i: (0, 0))],
        out_specs=rows,
        out_shape=jax.ShapeDtypeStruct(x.shape, bf16),
        compiler_params=grant(6),
        name="normalize",
    )(x, gain)


def project_kernel(normed_ref, own_ref, core_ref, far_ref, far_core_ref,
                   copies_ref, d_ref, proj_ref, emb_ref, q_ref, sems):
    depth = own_ref.shape[0]
    h, k = section_index()
    for ref, section in (
        (own_ref, h * 2 + k),
        (core_ref, h * 2 + 1 - k),
        (far_ref, (1 - h) * 2 + k),
        (far_core_ref, (1 - h) * 2 + 1 - k),
    ):
        emb_ref[pl.ds(pl.multiple_of(section * depth, depth), depth), :] = ref[...]
    pairs, _, _ = normed_ref.shape
    for p in range(pairs):
        projected = jnp.dot(normed_ref[p], emb_ref[...], preferred_element_type=f32)
        inverse_length = lax.rsqrt(
            jnp.sum(projected * projected, axis=-1, keepdims=True) + EPSILON
        )
        vectors = (projected * inverse_length).astype(bf16)
        q_ref[p * QLEN:(p + 1) * QLEN] = vectors[:QLEN]
        d_ref[p * DLEN:(p + 1) * DLEN] = vectors[QLEN:]
        proj_ref[p] = projected
    copies = [
        pltpu.make_async_copy(q_ref, copies_ref.at[n], sems.at[n])
        for n in range(copies_ref.shape[0])
    ]
    for copy in copies:
        copy.start()
    for copy in copies:
        copy.wait()


def project(normed, slices, readers):
    pairs, length, width = normed.shape
    _, features = slices[0].shape
    return pl.pallas_call(
        project_kernel,
        in_specs=[vmem()] * 5,
        out_specs=[hbm(), vmem(), vmem(), vmem()],
        out_shape=[
            pltpu.HBM((readers, pairs * QLEN, features), bf16),
            jax.ShapeDtypeStruct((pairs * DLEN, features), bf16),
            jax.ShapeDtypeStruct((pairs, length, features), f32),
            jax.ShapeDtypeStruct((width, features), bf16),
        ],
        scratch_shapes=[
            pltpu.VMEM((pairs * QLEN, features), bf16),
            pltpu.SemaphoreType.DMA((readers,)),
        ],
        compiler_params=grant(6),
        name="project",
    )(normed, *slices)


def micro_index():
    h, k = section_index()
    return h * 2 + k


def plane_index():
    return lax.axis_index("x") * lax.axis_size("y") + lax.axis_index("y")


def query_pair(holder, t, pairs):
    return (holder * lax.axis_size("z") + lax.axis_index("z")) * pairs + t


def document_pair(c, pairs, ring):
    z = lax.rem(lax.axis_index("z") - lax.div(c, pairs) + ring, ring)
    return (plane_index() * lax.axis_size("z") + z) * pairs + lax.rem(c, pairs)


def query_weights(request_ref, micro, holders, pairs):
    wide = pairs * QLEN
    lane = lax.broadcasted_iota(jnp.int32, (1, wide), 1)
    owner = lax.div(lane, QLEN)
    place = lane - owner * QLEN
    parts = []
    for holder in range(holders):
        span = jnp.zeros((1, wide), jnp.int32)
        for t in range(pairs):
            span = jnp.where(owner == t, request_ref[micro, query_pair(holder, t, pairs)], span)
        live = jnp.where(place < span, 1.0, 0.0).astype(f32)
        parts.append(live / span.astype(f32))
    return jnp.concatenate(parts, axis=1)


def matches(match_ref, micro, holders, pairs):
    lane = lax.broadcasted_iota(jnp.int32, (1, LANES), 1)
    match = jnp.full((1, LANES), -1, jnp.int32)
    for holder in range(holders):
        for t in range(pairs):
            match = jnp.where(
                lane == holder * pairs + t, match_ref[micro, query_pair(holder, t, pairs)], match
            )
    return match


def token_owners(lanes):
    first = lax.broadcasted_iota(jnp.int32, (lanes, LANES), 1) * QLEN
    ahead = lax.broadcasted_iota(jnp.int32, (lanes, LANES), 0) - first
    return jnp.where((ahead >= 0) & (ahead < QLEN), 1.0, 0.0).astype(bf16)


def parts_of(values):
    high = values.astype(bf16)
    rest = values - high.astype(f32)
    middle = rest.astype(bf16)
    low = (rest - middle.astype(f32)).astype(bf16)
    return low, middle, high


def sums_by_query(terms, owners):
    parts = [jnp.dot(part, owners, preferred_element_type=f32) for part in parts_of(terms)]
    return parts[0] + parts[1] + parts[2]


def given_to_tokens(values, owners):
    parts = [dot_nt(part, owners) for part in parts_of(values)]
    return parts[0] + parts[1] + parts[2]


def scores_kernel(pairs, request_ref, passage_ref, match_ref, steep_ref,
                  q_all, d0, d1, d2, d3,
                  docs_ref, level_ref, logits_ref, stats_ref, sim_a, sim_b):
    micro = micro_index()
    beta2 = steep_ref[0] * LOG2_E
    mult = steep_ref[1]
    arrived = (d0, d1, d2, d3)
    ring = len(arrived)
    own = d0.shape[0]
    for n, ref in enumerate(arrived):
        docs_ref[n * own:(n + 1) * own, :] = ref[...]
    lanes = q_all.shape[0]
    count = docs_ref.shape[0] // DLEN
    rows = GROUP * DLEN
    sims = (sim_a, sim_b)
    halves = count // GROUP
    token = lax.broadcasted_iota(jnp.int32, (DLEN - DLEN_LEAST, 1), 0) + DLEN_LEAST

    def spot(block):
        half, chunk = block % halves, block // halves
        return half * GROUP, slice(chunk * CHUNK, (chunk + 1) * CHUNK)

    def similarity(block, slot):
        c, at = spot(block)
        sims[slot][...] = dot_nt(docs_ref[c * DLEN:c * DLEN + rows, :], q_all[at, :])

    def pool(block, slot):
        ref = sims[slot]
        c, at = spot(block)
        levels = []
        for n in range(GROUP):
            span = passage_ref[micro, document_pair(c + n, pairs, ring)]
            row = n * DLEN
            early = ref[row:row + DLEN_LEAST, :]
            late = jnp.where(token < span, ref[row + DLEN_LEAST:row + DLEN, :], MASKED)
            highest = jnp.max(jnp.maximum(early, late), axis=0, keepdims=True)
            total = jnp.sum(
                jnp.exp2(beta2 * (early - highest)) + jnp.exp2(beta2 * (late - highest)),
                axis=0,
                keepdims=True,
            )
            levels.append(beta2 * highest + jnp.log2(total))
        level_ref[c:c + GROUP, at] = jnp.concatenate(levels, axis=0)

    in_turn(halves * (lanes // CHUNK), similarity, pool)

    holders = lanes // (pairs * QLEN)
    weight = query_weights(request_ref, micro, holders, pairs)
    smooth = level_ref[...] * (LN_2 / steep_ref[0])
    logits = mult * sums_by_query(smooth * weight, token_owners(lanes))
    logits_ref[...] = logits
    column = document_pair(lax.broadcasted_iota(jnp.int32, (count, 1), 0), pairs, ring)
    match = matches(match_ref, micro, holders, pairs)
    highest = jnp.max(logits, axis=0, keepdims=True)
    local = highest + jnp.log(jnp.sum(jnp.exp(logits - highest), axis=0, keepdims=True))
    positive = jnp.sum(jnp.where(column == match, logits, 0.0), axis=0, keepdims=True)
    tile = jnp.concatenate([local, positive, jnp.zeros((6, LANES), f32)], axis=0)
    for holder in range(holders):
        stats_ref[holder] = tile


def scores_forward(spans, steep, queries, docs, pairs):
    lanes, features = queries.shape
    rows = docs[0].shape[0] * len(docs)
    count = rows // DLEN
    holders = lanes // (pairs * QLEN)
    return pl.pallas_call(
        functools.partial(scores_kernel, pairs),
        in_specs=[smem()] * 4 + [vmem()] * 5,
        out_specs=[vmem()] * 4,
        out_shape=[
            jax.ShapeDtypeStruct((rows, features), bf16),
            jax.ShapeDtypeStruct((count, lanes), f32),
            jax.ShapeDtypeStruct((count, LANES), f32),
            jax.ShapeDtypeStruct((holders, 8, LANES), f32),
        ],
        scratch_shapes=[
            pltpu.VMEM((GROUP * DLEN, CHUNK), f32),
            pltpu.VMEM((GROUP * DLEN, CHUNK), f32),
        ],
        compiler_params=grant(10),
        name="scores_forward",
    )(*spans, steep, queries, *docs)


def slopes_kernel(pairs, ring, request_ref, passage_ref, match_ref, steep_ref,
                  docs_ref, q_all, level_ref, logits_ref, stats_ref,
                  gq_ref, gd0, gd1, gd2, gd3, loss_ref,
                  sim_a, sim_b, coef_ref, gq_vmem, sems):
    micro = micro_index()
    beta2 = steep_ref[0] * LOG2_E
    mult = steep_ref[1]
    lanes = q_all.shape[0]
    count = docs_ref.shape[0] // DLEN
    rows = GROUP * DLEN
    sims = (sim_a, sim_b)
    halves = count // GROUP
    holders = lanes // (pairs * QLEN)

    stats = stats_ref[...]
    locals_ = stats[:, 0, :]
    highest = jnp.max(locals_, axis=0, keepdims=True)
    log_total = highest + jnp.log(jnp.sum(jnp.exp(locals_ - highest), axis=0, keepdims=True))
    loss_ref[...] = log_total - jnp.sum(stats[:, 1, :], axis=0, keepdims=True)

    column = document_pair(lax.broadcasted_iota(jnp.int32, (count, 1), 0), pairs, ring)
    match = matches(match_ref, micro, holders, pairs)
    share = jnp.exp(logits_ref[...] - log_total) - jnp.where(column == match, 1.0, 0.0)
    slope = given_to_tokens(OBJECTIVE_FACTOR * mult * share, token_owners(lanes))
    coef_ref[...] = query_weights(request_ref, micro, holders, pairs) * slope

    token = lax.broadcasted_iota(jnp.int32, (DLEN - DLEN_LEAST, 1), 0) + DLEN_LEAST
    turned_parts = []
    sends = []
    gds = (gd0, gd1, gd2, gd3)
    own = gd0.shape[0]

    def spot(block):
        half, chunk = block % halves, block // halves
        return half * GROUP, slice(chunk * CHUNK, (chunk + 1) * CHUNK)

    def similarity(block, slot):
        c, at = spot(block)
        sims[slot][...] = dot_nt(docs_ref[c * DLEN:c * DLEN + rows, :], q_all[at, :])

    def weigh(block, slot):
        ref = sims[slot]
        c, at = spot(block)
        parts = []
        for n in range(GROUP):
            live = passage_ref[micro, document_pair(c + n, pairs, ring)]
            level = level_ref[c + n:c + n + 1, at]
            coef = coef_ref[c + n:c + n + 1, at]
            row = n * DLEN
            share = jnp.exp2(beta2 * ref[row:row + DLEN_LEAST, :] - level)
            parts.append((coef * share).astype(bf16))
            share = jnp.exp2(beta2 * ref[row + DLEN_LEAST:row + DLEN, :] - level)
            parts.append(jnp.where(token < live, coef * share, 0.0).astype(bf16))
        grad = jnp.concatenate(parts, axis=0)
        here = slice(c * DLEN, c * DLEN + rows)
        product = jnp.dot(grad, q_all[at, :], preferred_element_type=f32)
        for n in range(rows // own):
            ref = gds[c * DLEN // own + n]
            part = product[n * own:(n + 1) * own]
            ref[...] = part if block < halves else ref[...] + part
        turned_parts.append(dot_tn(docs_ref[here, :], grad))
        if len(turned_parts) == halves:
            total = functools.reduce(jnp.add, turned_parts)
            turned_parts.clear()
            gq_vmem[at, :] = total.T.astype(gq_vmem.dtype)
            send = pltpu.make_async_copy(
                gq_vmem.at[at], gq_ref.at[at], sems.at[block // halves]
            )
            send.start()
            sends.append(send)

    in_turn(halves * (lanes // CHUNK), similarity, weigh)
    for send in sends:
        send.wait()


def slopes(spans, steep, docs, queries, level, logits, stats, pairs, ring):
    lanes, features = queries.shape
    rows = docs.shape[0]
    return pl.pallas_call(
        functools.partial(slopes_kernel, pairs, ring),
        in_specs=[smem()] * 4 + [vmem()] * 5,
        out_specs=[hbm()] + [vmem()] * (ring + 1),
        out_shape=[
            pltpu.HBM((lanes, features), bf16),
            *[jax.ShapeDtypeStruct((rows // ring, features), f32)] * ring,
            jax.ShapeDtypeStruct((1, LANES), f32),
        ],
        scratch_shapes=[
            pltpu.VMEM((GROUP * DLEN, CHUNK), f32),
            pltpu.VMEM((GROUP * DLEN, CHUNK), f32),
            pltpu.VMEM(level.shape, f32),
            pltpu.VMEM((lanes, features), bf16),
            pltpu.SemaphoreType.DMA((lanes // CHUNK,)),
        ],
        compiler_params=grant(14),
        name="slopes",
    )(*spans, steep, docs, queries, level, logits, stats)


def head_backward_kernel(x_ref, gain_ref, emb_ref, proj_ref, gq_ref, g0, g1, g2, g3, out_ref,
                         out_vmem, sems):
    pairs = x_ref.shape[0]
    sends = []
    for p in range(pairs):
        at = slice(p * DLEN, (p + 1) * DLEN)
        grad_docs = g0[at] + g1[at] + g2[at] + g3[at]
        grad_query = jnp.sum(gq_ref[:, p * QLEN:(p + 1) * QLEN].astype(f32), axis=0)
        grad_vectors = jnp.concatenate([grad_query, grad_docs], axis=0)
        projected = proj_ref[p]
        inverse_length = lax.rsqrt(
            jnp.sum(projected * projected, axis=-1, keepdims=True) + EPSILON
        )
        unit = projected * inverse_length
        along = jnp.sum(unit * grad_vectors, axis=-1, keepdims=True)
        grad_projected = (inverse_length * (grad_vectors - unit * along)).astype(bf16)
        values = x_ref[p].astype(f32)
        inverse_rms = lax.rsqrt(jnp.mean(values * values, axis=-1, keepdims=True) + EPSILON)
        weighted = dot_nt(grad_projected, emb_ref[...]) * gain_ref[...]
        mean_term = jnp.mean(values * weighted, axis=-1, keepdims=True)
        out_vmem[p] = (
            inverse_rms * weighted
            - values * (inverse_rms * inverse_rms * inverse_rms) * mean_term
        ).astype(bf16)
        sends.append(pltpu.make_async_copy(out_vmem.at[p], out_ref.at[p], sems.at[p]))
        sends[-1].start()
    for send in sends:
        send.wait()


def head_backward(x, gain, emb, projected, grad_queries, grad_docs):
    pairs = x.shape[0]
    return pl.pallas_call(
        head_backward_kernel,
        in_specs=[vmem()] * 9,
        out_specs=hbm(),
        out_shape=jax.ShapeDtypeStruct(x.shape, bf16),
        scratch_shapes=[pltpu.VMEM(x.shape, bf16), pltpu.SemaphoreType.DMA((pairs,))],
        compiler_params=grant(10),
        name="head_backward",
    )(x, gain, emb, projected, grad_queries, *grad_docs)


def all_slices(own):
    swap = [(0, 1), (1, 0)]
    ring = lax.axis_size("z")
    mirror = [
        (h * ring + z, (1 - h) * ring + ring - 1 - z) for h in range(2) for z in range(ring)
    ]
    far = lax.ppermute(own, ("h", "z"), mirror)
    core = lax.ppermute(own, "k", swap)
    far_core = lax.ppermute(far, "k", swap)
    return own, core, far, far_core


def turned(array, shift):
    ring = lax.axis_size("z")
    return lax.ppermute(array, "z", [(i, (i + shift) % ring) for i in range(ring)])


def local(x, gain, embedding, request_span, passage_span, matching_pair, steepness):
    x = x[0]
    pairs = x.shape[0]
    ring = lax.axis_size("z")
    gain = gain[None]
    spans = (request_span, passage_span, matching_pair)
    plane = lax.axis_size(PLANE)

    def swapped(blocks):
        return lax.all_to_all(blocks, PLANE, split_axis=0, concat_axis=0, tiled=True)

    normed = normalize(x, gain)
    slices = all_slices(embedding)
    copies, d, projected, emb = project(normed, slices, plane)
    docs = [d] + [turned(d, s) for s in range(1, ring)]
    queries = swapped(copies)
    queries = queries.reshape(-1, queries.shape[-1])
    docs, level, logits, stats = scores_forward(spans, steepness, queries, docs, pairs)
    stats = swapped(stats)
    gq, *gd, loss = slopes(
        spans, steepness, docs, queries, level, logits, stats, pairs, ring
    )
    grad_docs = [gd[0]] + [turned(gd[s], -s) for s in range(1, ring)]
    grad_queries = swapped(gq.reshape(copies.shape))
    grad_x = head_backward(x, gain, emb, projected, grad_queries, grad_docs)
    own = lax.dynamic_slice_in_dim(loss, plane_index() * pairs, pairs, 1)
    return grad_x[None], own


def solution(mesh):
    side = round(mesh.shape["dp"] ** (1 / 3))
    finer = Mesh(mesh.devices.reshape(2, 2, side, side, side), ("h", "k", "x", "y", "z"))
    rows = P(SECTION, DP, None, None)
    return jax.shard_map(
        local,
        mesh=finer,
        in_specs=(rows, P(), P(SECTION, None), P(), P(), P(), P()),
        out_specs=(rows, P(SECTION, DP)),
        check_vma=False,
    )
```

time: 80.9 us -> 77.8 us (0.962)
  blocking collectives: 0 us -> 11.5 us
  starting transfers between devices: 30.6 us -> 24.3 us
  waiting for transfers between devices: 28.2 us -> 22.9 us
  local copies, waits for them, and re-layouts: 4.7 us -> 2.77 us
    all_to_all x2, waiting for transfers between devices: 13.7 us -> 1.87 us  [swapped(): lax.all_to_all(blocks, PLANE, split_axis=0, concat_axis=0, tiled=True)]
    all_to_all x0 -> x1, blocking collectives: none -> 11.5 us  [swapped(): lax.all_to_all(blocks, PLANE, split_axis=0, concat_axis=0, tiled=True)]
    ppermute x9 -> x6, waiting for transfers between devices: 8.02 us -> 14.5 us  [turned(): lax.ppermute(array, 'z', [(i, (i + shift) % ring) for i in range(ring)])]
    ppermute x9 -> x6, starting transfers between devices: 12 us -> 6.07 us  [turned(): lax.ppermute(array, 'z', [(i, (i + shift) % ring) for i in range(ring)])]
    pallas_call x3, Pallas kernels: 10.4 us -> 11.6 us  [the longest x1 5.8 us: slopes(): pl.pallas_call(functools.partial(slopes_kernel, pairs, ring), in_specs=[s...]
    pallas_call x1, Pallas kernels: 3.38 us -> 2.54 us  [head_backward(): pl.pallas_call(head_backward_kernel, in_specs=[vmem()] * 9, out_specs=hbm...]
    unnamed x21 -> x18, local copies, waits for them, and re-layouts: 2.83 us -> 2.19 us
  transfers between devices with their start and end apart: 14 -> 11, of which waited for: 8 -> 6; matrix products, arithmetic and copies ran while one was open for 4% -> 1% of each run, Pallas kernels for 1% -> 1%
where the time goes in v1:
time: 77.8 us; the launch traced here: 77.2 us
  starting transfers between devices  24.3 us (31%)
  waiting for transfers between devices  22.9 us (29%)
  Pallas kernels  14.9 us (19%)
  blocking collectives  11.5 us (15%)
  local copies, waits for them, and re-layouts  2.77 us (4%)
  between operations  0.92 us (1%)
    ppermute x6, waiting for transfers between devices, turned(): lax.ppermute(array, 'z', [(i, (i + shift) % ring) for i in range(ring)])  14.5 us
    all_to_all x2, starting transfers between devices, swapped(): lax.all_to_all(blocks, PLANE, split_axis=0, concat_axis=0, tiled=True)  12.2 us
    all_to_all x1, blocking collectives, swapped(): lax.all_to_all(blocks, PLANE, split_axis=0, concat_axis=0, tiled=True)  11.5 us
    ppermute x1, waiting for transfers between devices, all_slices(): far = lax.ppermute(own, ('h', 'z'), mirror)  6.51 us
    ppermute x6, starting transfers between devices, turned(): lax.ppermute(array, 'z', [(i, (i + shift) % ring) for i in range(ring)])  6.07 us
    ppermute x1, starting transfers between devices, all_slices(): far = lax.ppermute(own, ('h', 'z'), mirror)  5.94 us
    pallas_call x1, Pallas kernels, slopes(): pl.pallas_call(functools.partial(slopes_kernel, pairs, ring), in_specs=[s...  5.8 us
    pallas_call x1, Pallas kernels, scores_forward(): pl.pallas_call(functools.partial(scores_kernel, pairs), in_specs=[smem()]...  4.2 us
  transfers between devices with their start and end apart: 11, of which 6 were waited for; matrix products, arithmetic and copies ran while one was open for 1% of the time, Pallas kernels for 1%

profile of v1, /device:TPU:8, one launch (start us, length us, event | category | flops | bytes accessed | tf_op | source)
XLA Modules:
  0.0 77.2 jit_solution(9878350663975082919)
XLA Ops:
  0.6 5.9 %collective-permute-start.1 = (bf16[512,128]{1,0:T(8,128)(2,1)}, bf16[512,128]{1,0:T(8,128)(2,1)S(1)}, u32[]{:S(2)}, u32[]{:S(2)}) collective-permute-start(bf16[512,128]{1,0:T(8,128)(2,1)} %own_ref.1), channel_id=1, source_target_pairs={{0,131},{1,130},{2,129},{3,128},{128,3},{129,2},{130,1},{131,0},{4... | collective-permute-start | bytes 393224 | tf_op jit(solution)/shard_map/ppermute | solution.py:443
  6.6 0.0 collective-permute-start
  6.6 6.5 %collective-permute-done.1.far_ref = bf16[512,128]{1,0:T(8,128)(2,1)S(1)} collective-permute-done((bf16[512,128]{1,0:T(8,128)(2,1)}, bf16[512,128]{1,0:T(8,128)(2,1)S(1)}, u32[]{:S(2)}, u32[]{:S(2)}) %collective-permute-start.1) | collective-permute-done | bytes 131104 | tf_op jit(solution)/shard_map/ppermute | solution.py:443
  13.1 0.0 collective-permute-start.2
  13.1 0.0 copy-start
  13.1 1.4 %copy-done = bf16[1,4,96,2048]{3,2,1,0:T(8,128)(2,1)S(1)} copy-done((bf16[1,4,96,2048]{3,2,1,0:T(8,128)(2,1)S(1)}, bf16[1,4,96,2048]{3,2,1,0:T(8,128)(2,1)}, u32[]{:S(2)}) %copy-start) | copy-done | bytes 1572888
  14.5 0.0 copy-start.3
  14.5 0.7 copy-done.3
  15.2 0.0 copy-start.2
  15.2 0.8 %normalize.1.normed_ref = bf16[4,96,2048]{2,1,0:T(8,128)(2,1)S(1)} custom-call(bf16[4,96,2048]{2,1,0:T(8,128)(2,1)S(1)} %bitcast.5, f32[1,2048]{1,0:T(1,128)S(1)} %bitcast.9), custom_call_target="tpu_custom_call" | custom-call | tf_op jit(solution)/shard_map/normalize/pallas_call | solution.py:77
  16.0 0.0 copy-start.5
  16.0 0.0 copy-start.6
  16.0 0.0 copy-start.7
  16.0 0.0 copy-start.8
  16.0 0.0 collective-permute-done.core_ref
  16.0 0.0 collective-permute-done.2.far_core_ref
  16.1 0.0 copy-done.2
  16.1 1.6 %project.1 = (bf16[16,128,128]{2,1,0:T(8,128)(2,1)}, bf16[256,128]{1,0:T(8,128)(2,1)S(1)}, f32[4,96,128]{2,1,0:T(8,128)S(1)}, bf16[2048,128]{1,0:T(8,128)(2,1)S(1)}) custom-call(bf16[4,96,2048]{2,1,0:T(8,128)(2,1)S(1)} %normalize.1.normed_ref, bf16[512,128]{1,0:T(8,128)(2,1)S(1)} %copy-done.2, bf16[512,128]{1,0:T(8,128)(2,1)S(1)} %collective-permute-done.core_ref, ...), custom_call_target="tpu_custom_call" | custom-call | tf_op jit(solution)/shard_map/project/pallas_call | solution.py:122
  17.7 7.4 %all-to-all-start = ((bf16[16,128,128]{2,1,0:T(8,128)(2,1)}), bf16[16,128,128]{2,1,0:T(8,128)(2,1)S(1)}, u32[]{:S(2)}, u32[]{:S(2)}) async-start(bf16[16,128,128]{2,1,0:T(8,128)(2,1)} %get-tuple-element.18), calls=%async_computation | async-start | bytes 1048576 | tf_op jit(solution)/shard_map/all_to_all | solution.py:463
  25.1 0.0 copy-start.1
  25.1 0.0 copy-start.4
  25.1 2.0 %collective-permute-start.5 = (bf16[256,128]{1,0:T(8,128)(2,1)S(1)}, bf16[256,128]{1,0:T(8,128)(2,1)S(1)}, u32[]{:S(2)}, u32[]{:S(2)}) collective-permute-start(bf16[256,128]{1,0:T(8,128)(2,1)S(1)} %get-tuple-element.19.d0), channel_id=1, source_target_pairs={{0,3},{1,0},{2,1},{3,2},{4,7},{5,4},{6,5},{7,6},{8,11},{9,8},{10,9... | collective-permute-start | bytes 196616 | tf_op jit(solution)/shard_map/ppermute | solution.py:451
  27.1 0.0 collective-permute-start.4
  27.1 0.7 collective-permute-start.3
  27.8 1.8 %collective-permute-done.5.d3 = bf16[256,128]{1,0:T(8,128)(2,1)S(1)} collective-permute-done((bf16[256,128]{1,0:T(8,128)(2,1)S(1)}, bf16[256,128]{1,0:T(8,128)(2,1)S(1)}, u32[]{:S(2)}, u32[]{:S(2)}) %collective-permute-start.5) | collective-permute-done | bytes 65568 | tf_op jit(solution)/shard_map/ppermute | solution.py:451
  29.6 4.4 %collective-permute-done.4.d2 = bf16[256,128]{1,0:T(8,128)(2,1)S(1)} collective-permute-done((bf16[256,128]{1,0:T(8,128)(2,1)S(1)}, bf16[256,128]{1,0:T(8,128)(2,1)S(1)}, u32[]{:S(2)}, u32[]{:S(2)}) %collective-permute-start.4) | collective-permute-done | bytes 65568 | tf_op jit(solution)/shard_map/ppermute | solution.py:451
  34.1 0.0 collective-permute-done.3.d1
  34.1 1.9 %all-to-all-done = bf16[16,128,128]{2,1,0:T(8,128)(2,1)S(1)} async-done(((bf16[16,128,128]{2,1,0:T(8,128)(2,1)}), bf16[16,128,128]{2,1,0:T(8,128)(2,1)S(1)}, u32[]{:S(2)}, u32[]{:S(2)}) %all-to-all-start) | async-done | bytes 524320 | tf_op jit(solution)/shard_map/all_to_all | solution.py:463
  35.9 0.0 copy-done.5
  35.9 0.0 copy-done.6
  35.9 0.0 copy-done.7
  35.9 0.0 copy-done.8
  35.9 4.2 %scores_forward.1 = (bf16[1024,128]{1,0:T(8,128)(2,1)S(1)}, f32[16,2048]{1,0:T(8,128)S(1)}, f32[16,128]{1,0:T(8,128)S(1)}, f32[16,8,128]{2,1,0:T(8,128)S(1)}) custom-call(s32[4,256]{1,0:T(4,128)S(1)} %copy-done.5, s32[4,256]{1,0:T(4,128)S(1)} %copy-done.6, s32[4,256]{1,0:T(4,128)S(1)} %copy-done.7, f32[2]{0:T(128)S(1)} %copy-done.8, ...), custom_call_target="tpu_custom_call" | custom-call | tf_op jit(solution)/shard_map/scores_forward/pallas_call | solution.py:275
  40.2 11.5 %all_to_all.15.stats_ref = f32[16,8,128]{2,1,0:T(8,128)S(1)} all-to-all(f32[16,8,128]{2,1,0:T(8,128)S(1)} %get-tuple-element.23), channel_id=1, replica_groups=mesh['h'=2,'k'=2,'x'=4,'y'=4,'z'=4] {'x','y'}, dimensions={0} | all-to-all | bytes 131072 | tf_op jit(solution)/shard_map/all_to_all | solution.py:463
  51.6 5.8 %slopes.1 = (bf16[2048,128]{1,0:T(8,128)(2,1)}, f32[256,128]{1,0:T(8,128)S(1)}, f32[256,128]{1,0:T(8,128)}, f32[256,128]{1,0:T(8,128)}, f32[256,128]{1,0:T(8,128)S(1)}, /*index=5*/f32[1,128]{1,0:T(1,128)S(1)}) custom-call(s32[4,256]{1,0:T(4,128)S(1)} %copy-done.5, s32[4,256]{1,0:T(4,128)S(1)} %copy-done.6, s32[4,256]{1,0:T(4,128)S(1)} %copy-done.7, ...), custom_call_target="tpu_custom_call" | custom-call | tf_op jit(solution)/shard_map/slopes/pallas_call | solution.py:373
  57.4 4.8 %all-to-all-start.2 = ((bf16[16,128,128]{2,1,0:T(8,128)(2,1)}), bf16[16,128,128]{2,1,0:T(8,128)(2,1)S(1)}, u32[]{:S(2)}, u32[]{:S(2)}) async-start(bf16[16,128,128]{2,1,0:T(8,128)(2,1)} %bitcast.12), calls=%async_computation.2 | async-start | bytes 1048576 | tf_op jit(solution)/shard_map/all_to_all | solution.py:463
  62.3 1.5 %collective-permute-start.6 = (f32[256,128]{1,0:T(8,128)}, f32[256,128]{1,0:T(8,128)S(1)}, u32[]{:S(2)}, u32[]{:S(2)}) collective-permute-start(f32[256,128]{1,0:T(8,128)} %get-tuple-element.26), channel_id=1, source_target_pairs={{0,3},{1,0},{2,1},{3,2},{4,7},{5,4},{6,5},{7,6},{8,11},{9,8},{10,9... | collective-permute-start | bytes 393224 | tf_op jit(solution)/shard_map/ppermute | solution.py:451
  63.8 0.0 collective-permute-start.7
  63.8 1.9 %collective-permute-start.8 = (f32[256,128]{1,0:T(8,128)S(1)}, f32[256,128]{1,0:T(8,128)S(1)}, u32[]{:S(2)}, u32[]{:S(2)}) collective-permute-start(f32[256,128]{1,0:T(8,128)S(1)} %get-tuple-element.28), channel_id=1, source_target_pairs={{0,1},{1,2},{2,3},{3,0},{4,5},{5,6},{6,7},{7,4},{8,9},{9,10},{10,1... | collective-permute-start | bytes 393224 | tf_op jit(solution)/shard_map/ppermute | solution.py:451
  65.7 0.6 constant_dynamic-slice_fusion
  66.3 3.2 %collective-permute-done.6.g1 = f32[256,128]{1,0:T(8,128)S(1)} collective-permute-done((f32[256,128]{1,0:T(8,128)}, f32[256,128]{1,0:T(8,128)S(1)}, u32[]{:S(2)}, u32[]{:S(2)}) %collective-permute-start.6) | collective-permute-done | bytes 131104 | tf_op jit(solution)/shard_map/ppermute | solution.py:451
  69.5 5.0 %collective-permute-done.7.g2 = f32[256,128]{1,0:T(8,128)S(1)} collective-permute-done((f32[256,128]{1,0:T(8,128)}, f32[256,128]{1,0:T(8,128)S(1)}, u32[]{:S(2)}, u32[]{:S(2)}) %collective-permute-start.7) | collective-permute-done | bytes 131104 | tf_op jit(solution)/shard_map/ppermute | solution.py:451
  74.5 0.0 collective-permute-done.8.g3
  74.5 0.0 all-to-all-done.2.gq_ref
  74.5 0.0 copy-done.1
  74.5 0.0 copy-done.4
  74.5 2.5 %head_backward.1 = bf16[4,96,2048]{2,1,0:T(8,128)(2,1)} custom-call(bf16[4,96,2048]{2,1,0:T(8,128)(2,1)S(1)} %bitcast.6, f32[1,2048]{1,0:T(1,128)S(1)} %bitcast.10, bf16[2048,128]{1,0:T(8,128)(2,1)S(1)} %get-tuple-element.16.emb_ref, f32[4,96,128]{2,1,0:T(8,128)S(1)} %get-tuple-element.17.proj_ref, bf16[16,128,128]{2,1,0:T(8,128)(2,1)S(1)} %all-to-all-done.2.gq_ref, ...), custom_call_target="tpu_custom_call" | custom-call | tf_op jit(solution)/shard_map/head_backward/pallas_call | solution.py:426
Async XLA Ops:
  0.6 12.5 %collective-permute-start.1 = (bf16[512,128]{1,0:T(8,128)(2,1)}, bf16[512,128]{1,0:T(8,128)(2,1)S(1)}, u32[]{:S(2)}, u32[]{:S(2)}) collective-permute-start(bf16[512,128]{1,0:T(8,128)(2,1)} %own_ref.1), channel_id=1, source_target_pairs={{0,131},{1,130},{2,129},{3,128},{128,3},{129,2},{130,1},{131,0},{4... | collective-permute-start | bytes 393224 | tf_op jit(solution)/shard_map/ppermute | solution.py:443
  6.6 9.5 %collective-permute-start = (bf16[512,128]{1,0:T(8,128)(2,1)}, bf16[512,128]{1,0:T(8,128)(2,1)S(1)}, u32[]{:S(2)}, u32[]{:S(2)}) collective-permute-start(bf16[512,128]{1,0:T(8,128)(2,1)} %own_ref.1), channel_id=1, source_target_pairs={{0,64},{64,0},{1,65},{65,1},{2,66},{66,2},{3,67},{67,3},{4,68},{68... | collective-permute-start | bytes 393224 | tf_op jit(solution)/shard_map/ppermute | solution.py:444
  13.1 3.0 %collective-permute-start.2 = (bf16[512,128]{1,0:T(8,128)(2,1)S(1)}, bf16[512,128]{1,0:T(8,128)(2,1)S(1)}, u32[]{:S(2)}, u32[]{:S(2)}) collective-permute-start(bf16[512,128]{1,0:T(8,128)(2,1)S(1)} %collective-permute-done.1.far_ref), channel_id=1, source_target_pairs={{0,64},{64,0},{1,65},{65,1},{2,66},{66,2},{3,67},{67,3},{4,68},{68... | collective-permute-start | bytes 393224 | tf_op jit(solution)/shard_map/ppermute | solution.py:445
  13.1 1.4 %copy-start = (bf16[1,4,96,2048]{3,2,1,0:T(8,128)(2,1)S(1)}, bf16[1,4,96,2048]{3,2,1,0:T(8,128)(2,1)}, u32[]{:S(2)}) copy-start(bf16[1,4,96,2048]{3,2,1,0:T(8,128)(2,1)} %param.7) | copy-start | bytes 4718596
  14.5 0.7 copy-start.3
  15.2 0.9 %copy-start.2 = (bf16[512,128]{1,0:T(8,128)(2,1)S(1)}, bf16[512,128]{1,0:T(8,128)(2,1)}, u32[]{:S(2)}) copy-start(bf16[512,128]{1,0:T(8,128)(2,1)} %own_ref.1) | copy-start | bytes 393220
  16.0 19.9 %copy-start.5 = (s32[4,256]{1,0:T(4,128)S(1)}, s32[4,256]{1,0:T(4,128)}, u32[]{:S(2)}) copy-start(s32[4,256]{1,0:T(4,128)} %request_ref.3) | copy-start | bytes 12292
  16.0 19.9 %copy-start.6 = (s32[4,256]{1,0:T(4,128)S(1)}, s32[4,256]{1,0:T(4,128)}, u32[]{:S(2)}) copy-start(s32[4,256]{1,0:T(4,128)} %passage_ref.3) | copy-start | bytes 12292
  16.0 19.9 %copy-start.7 = (s32[4,256]{1,0:T(4,128)S(1)}, s32[4,256]{1,0:T(4,128)}, u32[]{:S(2)}) copy-start(s32[4,256]{1,0:T(4,128)} %match_ref.3) | copy-start | bytes 12292
  16.0 19.9 %copy-start.8 = (f32[2]{0:T(128)S(1)}, f32[2]{0:T(128)}, u32[]{:S(2)}) copy-start(f32[2]{0:T(128)} %steep_ref.3) | copy-start | bytes 28
  17.7 18.2 %all-to-all-start = ((bf16[16,128,128]{2,1,0:T(8,128)(2,1)}), bf16[16,128,128]{2,1,0:T(8,128)(2,1)S(1)}, u32[]{:S(2)}, u32[]{:S(2)}) async-start(bf16[16,128,128]{2,1,0:T(8,128)(2,1)} %get-tuple-element.18), calls=%async_computation | async-start | bytes 1048576 | tf_op jit(solution)/shard_map/all_to_all | solution.py:463
  25.1 49.4 %copy-start.1 = (bf16[1,4,96,2048]{3,2,1,0:T(8,128)(2,1)S(1)}, bf16[1,4,96,2048]{3,2,1,0:T(8,128)(2,1)}, u32[]{:S(2)}) copy-start(bf16[1,4,96,2048]{3,2,1,0:T(8,128)(2,1)} %param.7) | copy-start | bytes 4718596
  25.1 49.4 %copy-start.4 = (f32[2048]{0:T(1024)S(1)}, f32[2048]{0:T(1024)}, u32[]{:S(2)}) copy-start(f32[2048]{0:T(1024)} %param.8) | copy-start | bytes 24580
  25.1 4.5 %collective-permute-start.5 = (bf16[256,128]{1,0:T(8,128)(2,1)S(1)}, bf16[256,128]{1,0:T(8,128)(2,1)S(1)}, u32[]{:S(2)}, u32[]{:S(2)}) collective-permute-start(bf16[256,128]{1,0:T(8,128)(2,1)S(1)} %get-tuple-element.19.d0), channel_id=1, source_target_pairs={{0,3},{1,0},{2,1},{3,2},{4,7},{5,4},{6,5},{7,6},{8,11},{9,8},{10,9... | collective-permute-start | bytes 196616 | tf_op jit(solution)/shard_map/ppermute | solution.py:451
  27.1 6.9 %collective-permute-start.4 = (bf16[256,128]{1,0:T(8,128)(2,1)S(1)}, bf16[256,128]{1,0:T(8,128)(2,1)S(1)}, u32[]{:S(2)}, u32[]{:S(2)}) collective-permute-start(bf16[256,128]{1,0:T(8,128)(2,1)S(1)} %get-tuple-element.19.d0), channel_id=1, source_target_pairs={{0,2},{1,3},{2,0},{3,1},{4,6},{5,7},{6,4},{7,5},{8,10},{9,11},{10,... | collective-permute-start | bytes 196616 | tf_op jit(solution)/shard_map/ppermute | solution.py:451
  27.1 6.9 %collective-permute-start.3 = (bf16[256,128]{1,0:T(8,128)(2,1)S(1)}, bf16[256,128]{1,0:T(8,128)(2,1)S(1)}, u32[]{:S(2)}, u32[]{:S(2)}) collective-permute-start(bf16[256,128]{1,0:T(8,128)(2,1)S(1)} %get-tuple-element.19.d0), channel_id=1, source_target_pairs={{0,1},{1,2},{2,3},{3,0},{4,5},{5,6},{6,7},{7,4},{8,9},{9,10},{10,1... | collective-permute-start | bytes 196616 | tf_op jit(solution)/shard_map/ppermute | solution.py:451
  57.4 17.1 %all-to-all-start.2 = ((bf16[16,128,128]{2,1,0:T(8,128)(2,1)}), bf16[16,128,128]{2,1,0:T(8,128)(2,1)S(1)}, u32[]{:S(2)}, u32[]{:S(2)}) async-start(bf16[16,128,128]{2,1,0:T(8,128)(2,1)} %bitcast.12), calls=%async_computation.2 | async-start | bytes 1048576 | tf_op jit(solution)/shard_map/all_to_all | solution.py:463
  62.3 7.3 %collective-permute-start.6 = (f32[256,128]{1,0:T(8,128)}, f32[256,128]{1,0:T(8,128)S(1)}, u32[]{:S(2)}, u32[]{:S(2)}) collective-permute-start(f32[256,128]{1,0:T(8,128)} %get-tuple-element.26), channel_id=1, source_target_pairs={{0,3},{1,0},{2,1},{3,2},{4,7},{5,4},{6,5},{7,6},{8,11},{9,8},{10,9... | collective-permute-start | bytes 393224 | tf_op jit(solution)/shard_map/ppermute | solution.py:451
  63.8 10.7 %collective-permute-start.7 = (f32[256,128]{1,0:T(8,128)}, f32[256,128]{1,0:T(8,128)S(1)}, u32[]{:S(2)}, u32[]{:S(2)}) collective-permute-start(f32[256,128]{1,0:T(8,128)} %get-tuple-element.27), channel_id=1, source_target_pairs={{0,2},{1,3},{2,0},{3,1},{4,6},{5,7},{6,4},{7,5},{8,10},{9,11},{10,... | collective-permute-start | bytes 393224 | tf_op jit(solution)/shard_map/ppermute | solution.py:451
  63.8 10.7 %collective-permute-start.8 = (f32[256,128]{1,0:T(8,128)S(1)}, f32[256,128]{1,0:T(8,128)S(1)}, u32[]{:S(2)}, u32[]{:S(2)}) collective-permute-start(f32[256,128]{1,0:T(8,128)S(1)} %get-tuple-element.28), channel_id=1, source_target_pairs={{0,1},{1,2},{2,3},{3,0},{4,5},{5,6},{6,7},{7,4},{8,9},{9,10},{10,1... | collective-permute-start | bytes 393224 | tf_op jit(solution)/shard_map/ppermute | solution.py:451

commit v2 on v1

--- a/solution.py
+++ b/solution.py
@@ -13,6 +13,8 @@
 LANES = 128
 GROUP = 8
 CHUNK = 512
+CHUNK_F = 2048
+TOGETHER = 4
 DLEN_LEAST = 32
 SECTION = ("h", "k")
 PLANE = ("x", "y")
@@ -151,8 +153,8 @@
     return (holder * lax.axis_size("z") + lax.axis_index("z")) * pairs + t
 
 
-def document_pair(c, pairs, ring):
-    z = lax.rem(lax.axis_index("z") - lax.div(c, pairs) + ring, ring)
+def document_pair(c, pairs):
+    z = jnp.bitwise_xor(lax.axis_index("z"), lax.div(c, pairs))
     return (plane_index() * lax.axis_size("z") + z) * pairs + lax.rem(c, pairs)
 
 
@@ -182,9 +184,9 @@
     return match
 
 
-def token_owners(lanes):
-    first = lax.broadcasted_iota(jnp.int32, (lanes, LANES), 1) * QLEN
-    ahead = lax.broadcasted_iota(jnp.int32, (lanes, LANES), 0) - first
+def first_owners():
+    start = lax.broadcasted_iota(jnp.int32, (LANES, LANES), 0) * QLEN
+    ahead = lax.broadcasted_iota(jnp.int32, (LANES, LANES), 1) - start
     return jnp.where((ahead >= 0) & (ahead < QLEN), 1.0, 0.0).astype(bf16)
 
 
@@ -193,17 +195,32 @@
     rest = values - high.astype(f32)
     middle = rest.astype(bf16)
     low = (rest - middle.astype(f32)).astype(bf16)
-    return low, middle, high
-
-
-def sums_by_query(terms, owners):
-    parts = [jnp.dot(part, owners, preferred_element_type=f32) for part in parts_of(terms)]
-    return parts[0] + parts[1] + parts[2]
-
-
-def given_to_tokens(values, owners):
-    parts = [dot_nt(part, owners) for part in parts_of(values)]
-    return parts[0] + parts[1] + parts[2]
+    return jnp.concatenate([low, middle, high], axis=0)
+
+
+def joined(parts):
+    rows = parts.shape[0] // 3
+    return parts[:rows] + parts[rows:2 * rows] + parts[2 * rows:]
+
+
+def sums_by_query(terms, pairs):
+    wide = pairs * QLEN
+    owners = first_owners()
+    total = None
+    for holder in range(terms.shape[1] // wide):
+        sums = joined(dot_nt(parts_of(terms[:, holder * wide:(holder + 1) * wide]), owners))
+        sums = pltpu.roll(sums, holder * pairs, 1) if holder else sums
+        total = sums if total is None else total + sums
+    return total
+
+
+def given_to_tokens(values, holders, pairs):
+    owners = first_owners()
+    given = []
+    for holder in range(holders):
+        own = pltpu.roll(values, LANES - holder * pairs, 1) if holder else values
+        given.append(joined(jnp.dot(parts_of(own), owners, preferred_element_type=f32)))
+    return jnp.concatenate(given, axis=1)
 
 
 def scores_kernel(pairs, request_ref, passage_ref, match_ref, steep_ref,
@@ -213,7 +230,6 @@
     beta2 = steep_ref[0] * LOG2_E
     mult = steep_ref[1]
     arrived = (d0, d1, d2, d3)
-    ring = len(arrived)
     own = d0.shape[0]
     for n, ref in enumerate(arrived):
         docs_ref[n * own:(n + 1) * own, :] = ref[...]
@@ -226,7 +242,7 @@
 
     def spot(block):
         half, chunk = block % halves, block // halves
-        return half * GROUP, slice(chunk * CHUNK, (chunk + 1) * CHUNK)
+        return half * GROUP, slice(chunk * CHUNK_F, (chunk + 1) * CHUNK_F)
 
     def similarity(block, slot):
         c, at = spot(block)
@@ -237,7 +253,7 @@
         c, at = spot(block)
         levels = []
         for n in range(GROUP):
-            span = passage_ref[micro, document_pair(c + n, pairs, ring)]
+            span = passage_ref[micro, document_pair(c + n, pairs)]
             row = n * DLEN
             early = ref[row:row + DLEN_LEAST, :]
             late = jnp.where(token < span, ref[row + DLEN_LEAST:row + DLEN, :], MASKED)
@@ -250,14 +266,14 @@
             levels.append(beta2 * highest + jnp.log2(total))
         level_ref[c:c + GROUP, at] = jnp.concatenate(levels, axis=0)
 
-    in_turn(halves * (lanes // CHUNK), similarity, pool)
+    in_turn(halves * (lanes // CHUNK_F), similarity, pool)
 
     holders = lanes // (pairs * QLEN)
     weight = query_weights(request_ref, micro, holders, pairs)
     smooth = level_ref[...] * (LN_2 / steep_ref[0])
-    logits = mult * sums_by_query(smooth * weight, token_owners(lanes))
+    logits = mult * sums_by_query(smooth * weight, pairs)
     logits_ref[...] = logits
-    column = document_pair(lax.broadcasted_iota(jnp.int32, (count, 1), 0), pairs, ring)
+    column = document_pair(lax.broadcasted_iota(jnp.int32, (count, 1), 0), pairs)
     match = matches(match_ref, micro, holders, pairs)
     highest = jnp.max(logits, axis=0, keepdims=True)
     local = highest + jnp.log(jnp.sum(jnp.exp(logits - highest), axis=0, keepdims=True))
@@ -283,15 +299,15 @@
             jax.ShapeDtypeStruct((holders, 8, LANES), f32),
         ],
         scratch_shapes=[
-            pltpu.VMEM((GROUP * DLEN, CHUNK), f32),
-            pltpu.VMEM((GROUP * DLEN, CHUNK), f32),
+            pltpu.VMEM((GROUP * DLEN, CHUNK_F), f32),
+            pltpu.VMEM((GROUP * DLEN, CHUNK_F), f32),
         ],
         compiler_params=grant(10),
         name="scores_forward",
     )(*spans, steep, queries, *docs)
 
 
-def slopes_kernel(pairs, ring, request_ref, passage_ref, match_ref, steep_ref,
+def slopes_kernel(pairs, request_ref, passage_ref, match_ref, steep_ref,
                   docs_ref, q_all, level_ref, logits_ref, stats_ref,
                   gq_ref, gd0, gd1, gd2, gd3, loss_ref,
                   sim_a, sim_b, coef_ref, gq_vmem, sems):
@@ -311,10 +327,10 @@
     log_total = highest + jnp.log(jnp.sum(jnp.exp(locals_ - highest), axis=0, keepdims=True))
     loss_ref[...] = log_total - jnp.sum(stats[:, 1, :], axis=0, keepdims=True)
 
-    column = document_pair(lax.broadcasted_iota(jnp.int32, (count, 1), 0), pairs, ring)
+    column = document_pair(lax.broadcasted_iota(jnp.int32, (count, 1), 0), pairs)
     match = matches(match_ref, micro, holders, pairs)
     share = jnp.exp(logits_ref[...] - log_total) - jnp.where(column == match, 1.0, 0.0)
-    slope = given_to_tokens(OBJECTIVE_FACTOR * mult * share, token_owners(lanes))
+    slope = given_to_tokens(OBJECTIVE_FACTOR * mult * share, holders, pairs)
     coef_ref[...] = query_weights(request_ref, micro, holders, pairs) * slope
 
     token = lax.broadcasted_iota(jnp.int32, (DLEN - DLEN_LEAST, 1), 0) + DLEN_LEAST
@@ -336,7 +352,7 @@
         c, at = spot(block)
         parts = []
         for n in range(GROUP):
-            live = passage_ref[micro, document_pair(c + n, pairs, ring)]
+            live = passage_ref[micro, document_pair(c + n, pairs)]
             level = level_ref[c + n:c + n + 1, at]
             coef = coef_ref[c + n:c + n + 1, at]
             row = n * DLEN
@@ -371,7 +387,7 @@
     lanes, features = queries.shape
     rows = docs.shape[0]
     return pl.pallas_call(
-        functools.partial(slopes_kernel, pairs, ring),
+        functools.partial(slopes_kernel, pairs),
         in_specs=[smem()] * 4 + [vmem()] * 5,
         out_specs=[hbm()] + [vmem()] * (ring + 1),
         out_shape=[
@@ -395,28 +411,34 @@
                          out_vmem, sems):
     pairs = x_ref.shape[0]
     sends = []
-    for p in range(pairs):
-        at = slice(p * DLEN, (p + 1) * DLEN)
-        grad_docs = g0[at] + g1[at] + g2[at] + g3[at]
-        grad_query = jnp.sum(gq_ref[:, p * QLEN:(p + 1) * QLEN].astype(f32), axis=0)
-        grad_vectors = jnp.concatenate([grad_query, grad_docs], axis=0)
-        projected = proj_ref[p]
-        inverse_length = lax.rsqrt(
-            jnp.sum(projected * projected, axis=-1, keepdims=True) + EPSILON
-        )
-        unit = projected * inverse_length
-        along = jnp.sum(unit * grad_vectors, axis=-1, keepdims=True)
-        grad_projected = (inverse_length * (grad_vectors - unit * along)).astype(bf16)
-        values = x_ref[p].astype(f32)
-        inverse_rms = lax.rsqrt(jnp.mean(values * values, axis=-1, keepdims=True) + EPSILON)
-        weighted = dot_nt(grad_projected, emb_ref[...]) * gain_ref[...]
-        mean_term = jnp.mean(values * weighted, axis=-1, keepdims=True)
-        out_vmem[p] = (
-            inverse_rms * weighted
-            - values * (inverse_rms * inverse_rms * inverse_rms) * mean_term
-        ).astype(bf16)
-        sends.append(pltpu.make_async_copy(out_vmem.at[p], out_ref.at[p], sems.at[p]))
-        sends[-1].start()
+    for first in range(0, pairs, TOGETHER):
+        group = range(first, first + TOGETHER)
+        grads = []
+        for p in group:
+            at = slice(p * DLEN, (p + 1) * DLEN)
+            grad_docs = g0[at] + g1[at] + g2[at] + g3[at]
+            grad_query = jnp.sum(gq_ref[:, p * QLEN:(p + 1) * QLEN].astype(f32), axis=0)
+            grad_vectors = jnp.concatenate([grad_query, grad_docs], axis=0)
+            projected = proj_ref[p]
+            inverse_length = lax.rsqrt(
+                jnp.sum(projected * projected, axis=-1, keepdims=True) + EPSILON
+            )
+            unit = projected * inverse_length
+            along = jnp.sum(unit * grad_vectors, axis=-1, keepdims=True)
+            grads.append((inverse_length * (grad_vectors - unit * along)).astype(bf16))
+        normed = dot_nt(jnp.concatenate(grads, axis=0), emb_ref[...])
+        rows = normed.shape[0] // TOGETHER
+        for n, p in enumerate(group):
+            values = x_ref[p].astype(f32)
+            inverse_rms = lax.rsqrt(jnp.mean(values * values, axis=-1, keepdims=True) + EPSILON)
+            weighted = normed[n * rows:(n + 1) * rows] * gain_ref[...]
+            mean_term = jnp.mean(values * weighted, axis=-1, keepdims=True)
+            out_vmem[p] = (
+                inverse_rms * weighted
+                - values * (inverse_rms * inverse_rms * inverse_rms) * mean_term
+            ).astype(bf16)
+            sends.append(pltpu.make_async_copy(out_vmem.at[p], out_ref.at[p], sems.at[p]))
+            sends[-1].start()
     for send in sends:
         send.wait()
 
@@ -429,7 +451,7 @@
         out_specs=hbm(),
         out_shape=jax.ShapeDtypeStruct(x.shape, bf16),
         scratch_shapes=[pltpu.VMEM(x.shape, bf16), pltpu.SemaphoreType.DMA((pairs,))],
-        compiler_params=grant(10),
+        compiler_params=grant(14),
         name="head_backward",
     )(x, gain, emb, projected, grad_queries, *grad_docs)
 
@@ -446,9 +468,8 @@
     return own, core, far, far_core
 
 
-def turned(array, shift):
-    ring = lax.axis_size("z")
-    return lax.ppermute(array, "z", [(i, (i + shift) % ring) for i in range(ring)])
+def traded(array, step):
+    return lax.ppermute(array, "z", [(i, i ^ step) for i in range(lax.axis_size("z"))])
 
 
 def local(x, gain, embedding, request_span, passage_span, matching_pair, steepness):
@@ -465,7 +486,7 @@
     normed = normalize(x, gain)
     slices = all_slices(embedding)
     copies, d, projected, emb = project(normed, slices, plane)
-    docs = [d] + [turned(d, s) for s in range(1, ring)]
+    docs = [d] + [traded(d, s) for s in range(1, ring)]
     queries = swapped(copies)
     queries = queries.reshape(-1, queries.shape[-1])
     docs, level, logits, stats = scores_forward(spans, steepness, queries, docs, pairs)
@@ -473,7 +494,7 @@
     gq, *gd, loss = slopes(
         spans, steepness, docs, queries, level, logits, stats, pairs, ring
     )
-    grad_docs = [gd[0]] + [turned(gd[s], -s) for s in range(1, ring)]
+    grad_docs = [gd[0]] + [traded(gd[s], s) for s in range(1, ring)]
     grad_queries = swapped(gq.reshape(copies.shape))
     grad_x = head_backward(x, gain, emb, projected, grad_queries, grad_docs)
     own = lax.dynamic_slice_in_dim(loss, plane_index() * pairs, pairs, 1)

time: 77.8 us -> 76.2 us (0.979)
  waiting for transfers between devices: 22.9 us -> 19.9 us
  starting transfers between devices: 24.3 us -> 27.1 us
  Pallas kernels: 14.9 us -> 14 us
    ppermute x6, waiting for transfers between devices: 14.5 us -> 11.2 us  [traded(): lax.ppermute(array, 'z', [(i, i ^ step) for i in range(lax.axis_size('z'))])]
    ppermute x6, starting transfers between devices: 6.07 us -> 8.86 us  [traded(): lax.ppermute(array, 'z', [(i, i ^ step) for i in range(lax.axis_size('z'))])]
where the time goes in v2:
time: 76.2 us; the launch traced here: 75.6 us
  starting transfers between devices  27.1 us (36%)
  waiting for transfers between devices  19.9 us (26%)
  Pallas kernels  14 us (18%)
  blocking collectives  11.2 us (15%)
  local copies, waits for them, and re-layouts  2.77 us (4%)
    all_to_all x2, starting transfers between devices, swapped(): lax.all_to_all(blocks, PLANE, split_axis=0, concat_axis=0, tiled=True)  12.2 us
    ppermute x6, waiting for transfers between devices, traded(): lax.ppermute(array, 'z', [(i, i ^ step) for i in range(lax.axis_size('z'))])  11.2 us
    all_to_all x1, blocking collectives, swapped(): lax.all_to_all(blocks, PLANE, split_axis=0, concat_axis=0, tiled=True)  11.2 us
    ppermute x6, starting transfers between devices, traded(): lax.ppermute(array, 'z', [(i, i ^ step) for i in range(lax.axis_size('z'))])  8.86 us
    ppermute x1, waiting for transfers between devices, all_slices(): far = lax.ppermute(own, ('h', 'z'), mirror)  6.51 us
    ppermute x1, starting transfers between devices, all_slices(): far = lax.ppermute(own, ('h', 'z'), mirror)  5.94 us
    pallas_call x1, Pallas kernels, slopes(): pl.pallas_call(functools.partial(slopes_kernel, pairs), in_specs=[smem()]...  5.57 us
    pallas_call x1, Pallas kernels, scores_forward(): pl.pallas_call(functools.partial(scores_kernel, pairs), in_specs=[smem()]...  3.65 us
  transfers between devices with their start and end apart: 11, of which 6 were waited for; matrix products, arithmetic and copies ran while one was open for 1% of the time, Pallas kernels for 1%

profile of v2, /device:TPU:8, one launch (start us, length us, event | category | flops | bytes accessed | tf_op | source)
XLA Modules:
  0.0 75.6 jit_solution(6097674692503853979)
XLA Ops:
  0.6 5.9 %collective-permute-start.1 = (bf16[512,128]{1,0:T(8,128)(2,1)}, bf16[512,128]{1,0:T(8,128)(2,1)S(1)}, u32[]{:S(2)}, u32[]{:S(2)}) collective-permute-start(bf16[512,128]{1,0:T(8,128)(2,1)} %own_ref.1), channel_id=1, source_target_pairs={{0,131},{1,130},{2,129},{3,128},{128,3},{129,2},{130,1},{131,0},{4... | collective-permute-start | bytes 393224 | tf_op jit(solution)/shard_map/ppermute | solution.py:465
  6.6 0.0 collective-permute-start
  6.6 6.5 %collective-permute-done.1.far_ref = bf16[512,128]{1,0:T(8,128)(2,1)S(1)} collective-permute-done((bf16[512,128]{1,0:T(8,128)(2,1)}, bf16[512,128]{1,0:T(8,128)(2,1)S(1)}, u32[]{:S(2)}, u32[]{:S(2)}) %collective-permute-start.1) | collective-permute-done | bytes 131104 | tf_op jit(solution)/shard_map/ppermute | solution.py:465
  13.1 0.0 collective-permute-start.2
  13.1 0.0 copy-start
  13.1 1.4 %copy-done = bf16[1,4,96,2048]{3,2,1,0:T(8,128)(2,1)S(1)} copy-done((bf16[1,4,96,2048]{3,2,1,0:T(8,128)(2,1)S(1)}, bf16[1,4,96,2048]{3,2,1,0:T(8,128)(2,1)}, u32[]{:S(2)}) %copy-start) | copy-done | bytes 1572888
  14.5 0.0 copy-start.3
  14.5 0.7 copy-done.3
  15.2 0.0 copy-start.2
  15.2 0.8 %normalize.1.normed_ref = bf16[4,96,2048]{2,1,0:T(8,128)(2,1)S(1)} custom-call(bf16[4,96,2048]{2,1,0:T(8,128)(2,1)S(1)} %bitcast.5, f32[1,2048]{1,0:T(1,128)S(1)} %bitcast.9), custom_call_target="tpu_custom_call" | custom-call | tf_op jit(solution)/shard_map/normalize/pallas_call | solution.py:79
  16.0 0.0 copy-start.5
  16.0 0.0 copy-start.6
  16.0 0.0 copy-start.7
  16.0 0.0 copy-start.8
  16.0 0.0 collective-permute-done.core_ref
  16.0 0.0 collective-permute-done.2.far_core_ref
  16.1 0.0 copy-done.2
  16.1 1.6 %project.1 = (bf16[16,128,128]{2,1,0:T(8,128)(2,1)}, bf16[256,128]{1,0:T(8,128)(2,1)S(1)}, f32[4,96,128]{2,1,0:T(8,128)S(1)}, bf16[2048,128]{1,0:T(8,128)(2,1)S(1)}) custom-call(bf16[4,96,2048]{2,1,0:T(8,128)(2,1)S(1)} %normalize.1.normed_ref, bf16[512,128]{1,0:T(8,128)(2,1)S(1)} %copy-done.2, bf16[512,128]{1,0:T(8,128)(2,1)S(1)} %collective-permute-done.core_ref, ...), custom_call_target="tpu_custom_call" | custom-call | tf_op jit(solution)/shard_map/project/pallas_call | solution.py:124
  17.7 7.4 %all-to-all-start = ((bf16[16,128,128]{2,1,0:T(8,128)(2,1)}), bf16[16,128,128]{2,1,0:T(8,128)(2,1)S(1)}, u32[]{:S(2)}, u32[]{:S(2)}) async-start(bf16[16,128,128]{2,1,0:T(8,128)(2,1)} %get-tuple-element.18), calls=%async_computation | async-start | bytes 1048576 | tf_op jit(solution)/shard_map/all_to_all | solution.py:484
  25.1 0.0 copy-start.1
  25.1 0.0 copy-start.4
  25.1 2.0 %collective-permute-start.5 = (bf16[256,128]{1,0:T(8,128)(2,1)S(1)}, bf16[256,128]{1,0:T(8,128)(2,1)S(1)}, u32[]{:S(2)}, u32[]{:S(2)}) collective-permute-start(bf16[256,128]{1,0:T(8,128)(2,1)S(1)} %get-tuple-element.19.d0), channel_id=1, source_target_pairs={{0,3},{1,2},{2,1},{3,0},{4,7},{5,6},{6,5},{7,4},{8,11},{9,10},{10,... | collective-permute-start | bytes 196616 | tf_op jit(solution)/shard_map/ppermute | solution.py:472
  27.1 0.0 collective-permute-start.4
  27.1 2.5 %collective-permute-start.3 = (bf16[256,128]{1,0:T(8,128)(2,1)S(1)}, bf16[256,128]{1,0:T(8,128)(2,1)S(1)}, u32[]{:S(2)}, u32[]{:S(2)}) collective-permute-start(bf16[256,128]{1,0:T(8,128)(2,1)S(1)} %get-tuple-element.19.d0), channel_id=1, source_target_pairs={{0,1},{1,0},{2,3},{3,2},{4,5},{5,4},{6,7},{7,6},{8,9},{9,8},{10,11... | collective-permute-start | bytes 196616 | tf_op jit(solution)/shard_map/ppermute | solution.py:472
  29.6 2.3 %collective-permute-done.5.d3 = bf16[256,128]{1,0:T(8,128)(2,1)S(1)} collective-permute-done((bf16[256,128]{1,0:T(8,128)(2,1)S(1)}, bf16[256,128]{1,0:T(8,128)(2,1)S(1)}, u32[]{:S(2)}, u32[]{:S(2)}) %collective-permute-start.5) | collective-permute-done | bytes 65568 | tf_op jit(solution)/shard_map/ppermute | solution.py:472
  31.9 1.9 %collective-permute-done.4.d2 = bf16[256,128]{1,0:T(8,128)(2,1)S(1)} collective-permute-done((bf16[256,128]{1,0:T(8,128)(2,1)S(1)}, bf16[256,128]{1,0:T(8,128)(2,1)S(1)}, u32[]{:S(2)}, u32[]{:S(2)}) %collective-permute-start.4) | collective-permute-done | bytes 65568 | tf_op jit(solution)/shard_map/ppermute | solution.py:472
  33.8 0.0 collective-permute-done.3.d1
  33.8 2.1 %all-to-all-done = bf16[16,128,128]{2,1,0:T(8,128)(2,1)S(1)} async-done(((bf16[16,128,128]{2,1,0:T(8,128)(2,1)}), bf16[16,128,128]{2,1,0:T(8,128)(2,1)S(1)}, u32[]{:S(2)}, u32[]{:S(2)}) %all-to-all-start) | async-done | bytes 524320 | tf_op jit(solution)/shard_map/all_to_all | solution.py:484
  35.9 0.0 copy-done.5
  35.9 0.0 copy-done.6
  35.9 0.0 copy-done.7
  35.9 0.0 copy-done.8
  35.9 3.7 %scores_forward.1 = (bf16[1024,128]{1,0:T(8,128)(2,1)S(1)}, f32[16,2048]{1,0:T(8,128)S(1)}, f32[16,128]{1,0:T(8,128)S(1)}, f32[16,8,128]{2,1,0:T(8,128)S(1)}) custom-call(s32[4,256]{1,0:T(4,128)S(1)} %copy-done.5, s32[4,256]{1,0:T(4,128)S(1)} %copy-done.6, s32[4,256]{1,0:T(4,128)S(1)} %copy-done.7, f32[2]{0:T(128)S(1)} %copy-done.8, ...), custom_call_target="tpu_custom_call" | custom-call | tf_op jit(solution)/shard_map/scores_forward/pallas_call | solution.py:291
  39.6 11.2 %all_to_all.15.stats_ref = f32[16,8,128]{2,1,0:T(8,128)S(1)} all-to-all(f32[16,8,128]{2,1,0:T(8,128)S(1)} %get-tuple-element.23), channel_id=1, replica_groups=mesh['h'=2,'k'=2,'x'=4,'y'=4,'z'=4] {'x','y'}, dimensions={0} | all-to-all | bytes 131072 | tf_op jit(solution)/shard_map/all_to_all | solution.py:484
  50.8 5.6 %slopes.1 = (bf16[2048,128]{1,0:T(8,128)(2,1)}, f32[256,128]{1,0:T(8,128)S(1)}, f32[256,128]{1,0:T(8,128)}, f32[256,128]{1,0:T(8,128)}, f32[256,128]{1,0:T(8,128)S(1)}, /*index=5*/f32[1,128]{1,0:T(1,128)S(1)}) custom-call(s32[4,256]{1,0:T(4,128)S(1)} %copy-done.5, s32[4,256]{1,0:T(4,128)S(1)} %copy-done.6, s32[4,256]{1,0:T(4,128)S(1)} %copy-done.7, ...), custom_call_target="tpu_custom_call" | custom-call | tf_op jit(solution)/shard_map/slopes/pallas_call | solution.py:389
  56.4 4.8 %all-to-all-start.2 = ((bf16[16,128,128]{2,1,0:T(8,128)(2,1)}), bf16[16,128,128]{2,1,0:T(8,128)(2,1)S(1)}, u32[]{:S(2)}, u32[]{:S(2)}) async-start(bf16[16,128,128]{2,1,0:T(8,128)(2,1)} %bitcast.12), calls=%async_computation.2 | async-start | bytes 1048576 | tf_op jit(solution)/shard_map/all_to_all | solution.py:484
  61.2 0.1 collective-permute-start.6
  61.3 2.4 %collective-permute-start.7 = (f32[256,128]{1,0:T(8,128)}, f32[256,128]{1,0:T(8,128)S(1)}, u32[]{:S(2)}, u32[]{:S(2)}) collective-permute-start(f32[256,128]{1,0:T(8,128)} %get-tuple-element.27), channel_id=1, source_target_pairs={{0,2},{1,3},{2,0},{3,1},{4,6},{5,7},{6,4},{7,5},{8,10},{9,11},{10,... | collective-permute-start | bytes 393224 | tf_op jit(solution)/shard_map/ppermute | solution.py:472
  63.7 1.9 %collective-permute-start.8 = (f32[256,128]{1,0:T(8,128)S(1)}, f32[256,128]{1,0:T(8,128)S(1)}, u32[]{:S(2)}, u32[]{:S(2)}) collective-permute-start(f32[256,128]{1,0:T(8,128)S(1)} %get-tuple-element.28), channel_id=1, source_target_pairs={{0,3},{1,2},{2,1},{3,0},{4,7},{5,6},{6,5},{7,4},{8,11},{9,10},{10,... | collective-permute-start | bytes 393224 | tf_op jit(solution)/shard_map/ppermute | solution.py:472
  65.6 0.6 constant_dynamic-slice_fusion
  66.2 1.0 %collective-permute-done.6.g1 = f32[256,128]{1,0:T(8,128)S(1)} collective-permute-done((f32[256,128]{1,0:T(8,128)}, f32[256,128]{1,0:T(8,128)S(1)}, u32[]{:S(2)}, u32[]{:S(2)}) %collective-permute-start.6) | collective-permute-done | bytes 131104 | tf_op jit(solution)/shard_map/ppermute | solution.py:472
  67.2 6.0 %collective-permute-done.7.g2 = f32[256,128]{1,0:T(8,128)S(1)} collective-permute-done((f32[256,128]{1,0:T(8,128)}, f32[256,128]{1,0:T(8,128)S(1)}, u32[]{:S(2)}, u32[]{:S(2)}) %collective-permute-start.7) | collective-permute-done | bytes 131104 | tf_op jit(solution)/shard_map/ppermute | solution.py:472
  73.2 0.0 collective-permute-done.8.g3
  73.2 0.0 all-to-all-done.2.gq_ref
  73.2 0.0 copy-done.1
  73.3 0.0 copy-done.4
  73.3 2.4 %head_backward.1 = bf16[4,96,2048]{2,1,0:T(8,128)(2,1)} custom-call(bf16[4,96,2048]{2,1,0:T(8,128)(2,1)S(1)} %bitcast.6, f32[1,2048]{1,0:T(1,128)S(1)} %bitcast.10, bf16[2048,128]{1,0:T(8,128)(2,1)S(1)} %get-tuple-element.16.emb_ref, f32[4,96,128]{2,1,0:T(8,128)S(1)} %get-tuple-element.17.proj_ref, bf16[16,128,128]{2,1,0:T(8,128)(2,1)S(1)} %all-to-all-done.2.gq_ref, ...), custom_call_target="tpu_custom_call" | custom-call | tf_op jit(solution)/shard_map/head_backward/pallas_call | solution.py:448
Async XLA Ops:
  0.6 12.5 %collective-permute-start.1 = (bf16[512,128]{1,0:T(8,128)(2,1)}, bf16[512,128]{1,0:T(8,128)(2,1)S(1)}, u32[]{:S(2)}, u32[]{:S(2)}) collective-permute-start(bf16[512,128]{1,0:T(8,128)(2,1)} %own_ref.1), channel_id=1, source_target_pairs={{0,131},{1,130},{2,129},{3,128},{128,3},{129,2},{130,1},{131,0},{4... | collective-permute-start | bytes 393224 | tf_op jit(solution)/shard_map/ppermute | solution.py:465
  6.6 9.5 %collective-permute-start = (bf16[512,128]{1,0:T(8,128)(2,1)}, bf16[512,128]{1,0:T(8,128)(2,1)S(1)}, u32[]{:S(2)}, u32[]{:S(2)}) collective-permute-start(bf16[512,128]{1,0:T(8,128)(2,1)} %own_ref.1), channel_id=1, source_target_pairs={{0,64},{64,0},{1,65},{65,1},{2,66},{66,2},{3,67},{67,3},{4,68},{68... | collective-permute-start | bytes 393224 | tf_op jit(solution)/shard_map/ppermute | solution.py:466
  13.1 3.0 %collective-permute-start.2 = (bf16[512,128]{1,0:T(8,128)(2,1)S(1)}, bf16[512,128]{1,0:T(8,128)(2,1)S(1)}, u32[]{:S(2)}, u32[]{:S(2)}) collective-permute-start(bf16[512,128]{1,0:T(8,128)(2,1)S(1)} %collective-permute-done.1.far_ref), channel_id=1, source_target_pairs={{0,64},{64,0},{1,65},{65,1},{2,66},{66,2},{3,67},{67,3},{4,68},{68... | collective-permute-start | bytes 393224 | tf_op jit(solution)/shard_map/ppermute | solution.py:467
  13.1 1.4 %copy-start = (bf16[1,4,96,2048]{3,2,1,0:T(8,128)(2,1)S(1)}, bf16[1,4,96,2048]{3,2,1,0:T(8,128)(2,1)}, u32[]{:S(2)}) copy-start(bf16[1,4,96,2048]{3,2,1,0:T(8,128)(2,1)} %param.7) | copy-start | bytes 4718596
  14.5 0.7 copy-start.3
  15.2 0.9 %copy-start.2 = (bf16[512,128]{1,0:T(8,128)(2,1)S(1)}, bf16[512,128]{1,0:T(8,128)(2,1)}, u32[]{:S(2)}) copy-start(bf16[512,128]{1,0:T(8,128)(2,1)} %own_ref.1) | copy-start | bytes 393220
  16.0 19.9 %copy-start.5 = (s32[4,256]{1,0:T(4,128)S(1)}, s32[4,256]{1,0:T(4,128)}, u32[]{:S(2)}) copy-start(s32[4,256]{1,0:T(4,128)} %request_ref.3) | copy-start | bytes 12292
  16.0 19.9 %copy-start.6 = (s32[4,256]{1,0:T(4,128)S(1)}, s32[4,256]{1,0:T(4,128)}, u32[]{:S(2)}) copy-start(s32[4,256]{1,0:T(4,128)} %passage_ref.3) | copy-start | bytes 12292
  16.0 19.9 %copy-start.7 = (s32[4,256]{1,0:T(4,128)S(1)}, s32[4,256]{1,0:T(4,128)}, u32[]{:S(2)}) copy-start(s32[4,256]{1,0:T(4,128)} %match_ref.3) | copy-start | bytes 12292
  16.0 19.9 %copy-start.8 = (f32[2]{0:T(128)S(1)}, f32[2]{0:T(128)}, u32[]{:S(2)}) copy-start(f32[2]{0:T(128)} %steep_ref.3) | copy-start | bytes 28
  17.7 18.2 %all-to-all-start = ((bf16[16,128,128]{2,1,0:T(8,128)(2,1)}), bf16[16,128,128]{2,1,0:T(8,128)(2,1)S(1)}, u32[]{:S(2)}, u32[]{:S(2)}) async-start(bf16[16,128,128]{2,1,0:T(8,128)(2,1)} %get-tuple-element.18), calls=%async_computation | async-start | bytes 1048576 | tf_op jit(solution)/shard_map/all_to_all | solution.py:484
  25.1 48.1 %copy-start.1 = (bf16[1,4,96,2048]{3,2,1,0:T(8,128)(2,1)S(1)}, bf16[1,4,96,2048]{3,2,1,0:T(8,128)(2,1)}, u32[]{:S(2)}) copy-start(bf16[1,4,96,2048]{3,2,1,0:T(8,128)(2,1)} %param.7) | copy-start | bytes 4718596
  25.1 48.1 %copy-start.4 = (f32[2048]{0:T(1024)S(1)}, f32[2048]{0:T(1024)}, u32[]{:S(2)}) copy-start(f32[2048]{0:T(1024)} %param.8) | copy-start | bytes 24580
  25.1 6.7 %collective-permute-start.5 = (bf16[256,128]{1,0:T(8,128)(2,1)S(1)}, bf16[256,128]{1,0:T(8,128)(2,1)S(1)}, u32[]{:S(2)}, u32[]{:S(2)}) collective-permute-start(bf16[256,128]{1,0:T(8,128)(2,1)S(1)} %get-tuple-element.19.d0), channel_id=1, source_target_pairs={{0,3},{1,2},{2,1},{3,0},{4,7},{5,6},{6,5},{7,4},{8,11},{9,10},{10,... | collective-permute-start | bytes 196616 | tf_op jit(solution)/shard_map/ppermute | solution.py:472
  27.1 6.7 %collective-permute-start.4 = (bf16[256,128]{1,0:T(8,128)(2,1)S(1)}, bf16[256,128]{1,0:T(8,128)(2,1)S(1)}, u32[]{:S(2)}, u32[]{:S(2)}) collective-permute-start(bf16[256,128]{1,0:T(8,128)(2,1)S(1)} %get-tuple-element.19.d0), channel_id=1, source_target_pairs={{0,2},{1,3},{2,0},{3,1},{4,6},{5,7},{6,4},{7,5},{8,10},{9,11},{10,... | collective-permute-start | bytes 196616 | tf_op jit(solution)/shard_map/ppermute | solution.py:472
  27.1 6.7 %collective-permute-start.3 = (bf16[256,128]{1,0:T(8,128)(2,1)S(1)}, bf16[256,128]{1,0:T(8,128)(2,1)S(1)}, u32[]{:S(2)}, u32[]{:S(2)}) collective-permute-start(bf16[256,128]{1,0:T(8,128)(2,1)S(1)} %get-tuple-element.19.d0), channel_id=1, source_target_pairs={{0,1},{1,0},{2,3},{3,2},{4,5},{5,4},{6,7},{7,6},{8,9},{9,8},{10,11... | collective-permute-start | bytes 196616 | tf_op jit(solution)/shard_map/ppermute | solution.py:472
  56.4 16.9 %all-to-all-start.2 = ((bf16[16,128,128]{2,1,0:T(8,128)(2,1)}), bf16[16,128,128]{2,1,0:T(8,128)(2,1)S(1)}, u32[]{:S(2)}, u32[]{:S(2)}) async-start(bf16[16,128,128]{2,1,0:T(8,128)(2,1)} %bitcast.12), calls=%async_computation.2 | async-start | bytes 1048576 | tf_op jit(solution)/shard_map/all_to_all | solution.py:484
  61.2 6.0 %collective-permute-start.6 = (f32[256,128]{1,0:T(8,128)}, f32[256,128]{1,0:T(8,128)S(1)}, u32[]{:S(2)}, u32[]{:S(2)}) collective-permute-start(f32[256,128]{1,0:T(8,128)} %get-tuple-element.26), channel_id=1, source_target_pairs={{0,1},{1,0},{2,3},{3,2},{4,5},{5,4},{6,7},{7,6},{8,9},{9,8},{10,11... | collective-permute-start | bytes 393224 | tf_op jit(solution)/shard_map/ppermute | solution.py:472
  61.3 11.9 %collective-permute-start.7 = (f32[256,128]{1,0:T(8,128)}, f32[256,128]{1,0:T(8,128)S(1)}, u32[]{:S(2)}, u32[]{:S(2)}) collective-permute-start(f32[256,128]{1,0:T(8,128)} %get-tuple-element.27), channel_id=1, source_target_pairs={{0,2},{1,3},{2,0},{3,1},{4,6},{5,7},{6,4},{7,5},{8,10},{9,11},{10,... | collective-permute-start | bytes 393224 | tf_op jit(solution)/shard_map/ppermute | solution.py:472
  63.7 9.6 %collective-permute-start.8 = (f32[256,128]{1,0:T(8,128)S(1)}, f32[256,128]{1,0:T(8,128)S(1)}, u32[]{:S(2)}, u32[]{:S(2)}) collective-permute-start(f32[256,128]{1,0:T(8,128)S(1)} %get-tuple-element.28), channel_id=1, source_target_pairs={{0,3},{1,2},{2,1},{3,0},{4,7},{5,6},{6,5},{7,4},{8,11},{9,10},{10,... | collective-permute-start | bytes 393224 | tf_op jit(solution)/shard_map/ppermute | solution.py:472

commit v3 on v2

--- a/solution.py
+++ b/solution.py
@@ -87,20 +87,41 @@
     )(x, gain)
 
 
-def project_kernel(normed_ref, own_ref, core_ref, far_ref, far_core_ref,
-                   copies_ref, d_ref, proj_ref, emb_ref, q_ref, sems):
+def section_rows(depth, far, other):
+    h, k = section_index()
+    section = (1 - h if far else h) * 2 + (1 - k if other else k)
+    return pl.ds(pl.multiple_of(section * depth, depth), depth)
+
+
+def partial_kernel(normed_ref, own_ref, core_ref, far_ref, part_ref):
     depth = own_ref.shape[0]
-    h, k = section_index()
-    for ref, section in (
-        (own_ref, h * 2 + k),
-        (core_ref, h * 2 + 1 - k),
-        (far_ref, (1 - h) * 2 + k),
-        (far_core_ref, (1 - h) * 2 + 1 - k),
-    ):
-        emb_ref[pl.ds(pl.multiple_of(section * depth, depth), depth), :] = ref[...]
-    pairs, _, _ = normed_ref.shape
-    for p in range(pairs):
-        projected = jnp.dot(normed_ref[p], emb_ref[...], preferred_element_type=f32)
+    for p in range(normed_ref.shape[0]):
+        part_ref[p] = sum(
+            jnp.dot(normed_ref[p, :, section_rows(depth, far, other)], ref[...],
+                    preferred_element_type=f32)
+            for ref, far, other in ((own_ref, 0, 0), (core_ref, 0, 1), (far_ref, 1, 0))
+        )
+
+
+def project_partly(normed, own, core, far):
+    pairs, length, _ = normed.shape
+    return pl.pallas_call(
+        partial_kernel,
+        in_specs=[vmem()] * 4,
+        out_specs=vmem(),
+        out_shape=jax.ShapeDtypeStruct((pairs, length, own.shape[1]), f32),
+        compiler_params=grant(6),
+        name="project_partly",
+    )(normed, own, core, far)
+
+
+def project_kernel(normed_ref, part_ref, last_ref, copies_ref, d_ref, proj_ref, q_ref, sems):
+    depth = last_ref.shape[0]
+    for p in range(normed_ref.shape[0]):
+        projected = part_ref[p] + jnp.dot(
+            normed_ref[p, :, section_rows(depth, 1, 1)], last_ref[...],
+            preferred_element_type=f32,
+        )
         inverse_length = lax.rsqrt(
             jnp.sum(projected * projected, axis=-1, keepdims=True) + EPSILON
         )
@@ -118,18 +139,17 @@
         copy.wait()
 
 
-def project(normed, slices, readers):
-    pairs, length, width = normed.shape
-    _, features = slices[0].shape
+def project(normed, part, last, readers):
+    pairs, length, _ = normed.shape
+    features = last.shape[1]
     return pl.pallas_call(
         project_kernel,
-        in_specs=[vmem()] * 5,
-        out_specs=[hbm(), vmem(), vmem(), vmem()],
+        in_specs=[vmem()] * 3,
+        out_specs=[hbm(), vmem(), vmem()],
         out_shape=[
             pltpu.HBM((readers, pairs * QLEN, features), bf16),
             jax.ShapeDtypeStruct((pairs * DLEN, features), bf16),
             jax.ShapeDtypeStruct((pairs, length, features), f32),
-            jax.ShapeDtypeStruct((width, features), bf16),
         ],
         scratch_shapes=[
             pltpu.VMEM((pairs * QLEN, features), bf16),
@@ -137,7 +157,27 @@
         ],
         compiler_params=grant(6),
         name="project",
-    )(normed, *slices)
+    )(normed, part, last)
+
+
+def assemble_kernel(own_ref, core_ref, far_ref, far_core_ref, emb_ref):
+    depth = own_ref.shape[0]
+    emb_ref[section_rows(depth, 0, 0), :] = own_ref[...]
+    emb_ref[section_rows(depth, 0, 1), :] = core_ref[...]
+    emb_ref[section_rows(depth, 1, 0), :] = far_ref[...]
+    emb_ref[section_rows(depth, 1, 1), :] = far_core_ref[...]
+
+
+def assemble(slices):
+    depth, features = slices[0].shape
+    return pl.pallas_call(
+        assemble_kernel,
+        in_specs=[vmem()] * 4,
+        out_specs=vmem(),
+        out_shape=jax.ShapeDtypeStruct((depth * len(slices), features), bf16),
+        compiler_params=grant(4),
+        name="assemble",
+    )(*slices)
 
 
 def micro_index():
@@ -485,7 +525,9 @@
 
     normed = normalize(x, gain)
     slices = all_slices(embedding)
-    copies, d, projected, emb = project(normed, slices, plane)
+    part = project_partly(normed, *slices[:3])
+    copies, d, projected = project(normed, part, slices[3], plane)
+    emb = assemble(slices)
     docs = [d] + [traded(d, s) for s in range(1, ring)]
     queries = swapped(copies)
     queries = queries.reshape(-1, queries.shape[-1])

time: 76.2 us -> 77.6 us (1.018)
  Pallas kernels: 14 us -> 15.3 us
    pallas_call x1, Pallas kernels: 2.38 us -> 3.42 us  [head_backward(): pl.pallas_call(head_backward_kernel, in_specs=[vmem()] * 9, out_specs=hbm...]
    pallas_call x1 -> x3, Pallas kernels: 1.61 us -> 1.76 us  [the longest x1 1.25 us: project(): pl.pallas_call(project_kernel, in_specs=[vmem()] * 3, out_specs=[hbm(), v...]
  transfers between devices with their start and end apart: 11 -> 11, of which waited for: 6 -> 6; matrix products, arithmetic and copies ran while one was open for 1% -> 1% of each run, Pallas kernels for 1% -> 2%
where the time goes in v3:
time: 77.6 us; the launch traced here: 77 us
  starting transfers between devices  27 us (35%)
  waiting for transfers between devices  20 us (26%)
  Pallas kernels  15.3 us (20%)
  blocking collectives  11.1 us (14%)
  local copies, waits for them, and re-layouts  2.83 us (4%)
    all_to_all x2, starting transfers between devices, swapped(): lax.all_to_all(blocks, PLANE, split_axis=0, concat_axis=0, tiled=True)  12.2 us
    ppermute x6, waiting for transfers between devices, traded(): lax.ppermute(array, 'z', [(i, i ^ step) for i in range(lax.axis_size('z'))])  11.3 us
    all_to_all x1, blocking collectives, swapped(): lax.all_to_all(blocks, PLANE, split_axis=0, concat_axis=0, tiled=True)  11.1 us
    ppermute x6, starting transfers between devices, traded(): lax.ppermute(array, 'z', [(i, i ^ step) for i in range(lax.axis_size('z'))])  8.77 us
    ppermute x1, waiting for transfers between devices, all_slices(): far = lax.ppermute(own, ('h', 'z'), mirror)  6.51 us
    ppermute x1, starting transfers between devices, all_slices(): far = lax.ppermute(own, ('h', 'z'), mirror)  5.94 us
    pallas_call x1, Pallas kernels, slopes(): pl.pallas_call(functools.partial(slopes_kernel, pairs), in_specs=[smem()]...  5.65 us
    pallas_call x1, Pallas kernels, scores_forward(): pl.pallas_call(functools.partial(scores_kernel, pairs), in_specs=[smem()]...  3.67 us
  transfers between devices with their start and end apart: 11, of which 6 were waited for; matrix products, arithmetic and copies ran while one was open for 1% of the time, Pallas kernels for 2%

profile of v3, /device:TPU:8, one launch (start us, length us, event | category | flops | bytes accessed | tf_op | source)
XLA Modules:
  0.0 77.0 jit_solution(1903420455751922299)
XLA Ops:
  0.6 5.9 %collective-permute-start.1 = (bf16[512,128]{1,0:T(8,128)(2,1)}, bf16[512,128]{1,0:T(8,128)(2,1)S(1)}, u32[]{:S(2)}, u32[]{:S(2)}) collective-permute-start(bf16[512,128]{1,0:T(8,128)(2,1)} %own_ref.3), channel_id=1, source_target_pairs={{0,131},{1,130},{2,129},{3,128},{128,3},{129,2},{130,1},{131,0},{4... | collective-permute-start | bytes 393224 | tf_op jit(solution)/shard_map/ppermute | solution.py:505
  6.6 0.0 collective-permute-start
  6.6 6.5 %collective-permute-done.1.far_ref = bf16[512,128]{1,0:T(8,128)(2,1)S(1)} collective-permute-done((bf16[512,128]{1,0:T(8,128)(2,1)}, bf16[512,128]{1,0:T(8,128)(2,1)S(1)}, u32[]{:S(2)}, u32[]{:S(2)}) %collective-permute-start.1) | collective-permute-done | bytes 131104 | tf_op jit(solution)/shard_map/ppermute | solution.py:505
  13.1 0.0 collective-permute-start.2
  13.1 0.0 copy-start
  13.1 1.4 %copy-done = bf16[1,4,96,2048]{3,2,1,0:T(8,128)(2,1)S(1)} copy-done((bf16[1,4,96,2048]{3,2,1,0:T(8,128)(2,1)S(1)}, bf16[1,4,96,2048]{3,2,1,0:T(8,128)(2,1)}, u32[]{:S(2)}) %copy-start) | copy-done | bytes 1572888
  14.5 0.0 copy-start.3
  14.5 0.7 copy-done.3
  15.2 0.0 copy-start.2
  15.2 0.8 %normalize.1.normed_ref = bf16[4,96,2048]{2,1,0:T(8,128)(2,1)S(1)} custom-call(bf16[4,96,2048]{2,1,0:T(8,128)(2,1)S(1)} %bitcast.5, f32[1,2048]{1,0:T(1,128)S(1)} %bitcast.9), custom_call_target="tpu_custom_call" | custom-call | tf_op jit(solution)/shard_map/normalize/pallas_call | solution.py:79
  16.0 0.0 collective-permute-done.core_ref
  16.0 0.1 copy-done.2
  16.1 0.5 project_partly.1.part_ref
  16.6 0.0 copy-start.5
  16.6 0.0 copy-start.6
  16.6 0.0 copy-start.7
  16.6 0.0 copy-start.8
  16.6 0.0 collective-permute-done.2.far_core_ref.last_ref
  16.6 1.2 %project.1 = (bf16[16,128,128]{2,1,0:T(8,128)(2,1)}, bf16[256,128]{1,0:T(8,128)(2,1)S(1)}, f32[4,96,128]{2,1,0:T(8,128)S(1)}) custom-call(bf16[4,96,2048]{2,1,0:T(8,128)(2,1)S(1)} %normalize.1.normed_ref, f32[4,96,128]{2,1,0:T(8,128)S(1)} %project_partly.1.part_ref, bf16[512,128]{1,0:T(8,128)(2,1)S(1)} %collective-permute-done.2.far_core_ref.last_ref), custom_call_target="tpu_custom_call" | custom-call | tf_op jit(solution)/shard_map/project/pallas_call | solution.py:145
  17.9 7.4 %all-to-all-start = ((bf16[16,128,128]{2,1,0:T(8,128)(2,1)}), bf16[16,128,128]{2,1,0:T(8,128)(2,1)S(1)}, u32[]{:S(2)}, u32[]{:S(2)}) async-start(bf16[16,128,128]{2,1,0:T(8,128)(2,1)} %get-tuple-element.16), calls=%async_computation | async-start | bytes 1048576 | tf_op jit(solution)/shard_map/all_to_all | solution.py:524
  25.3 1.9 %collective-permute-start.5 = (bf16[256,128]{1,0:T(8,128)(2,1)S(1)}, bf16[256,128]{1,0:T(8,128)(2,1)S(1)}, u32[]{:S(2)}, u32[]{:S(2)}) collective-permute-start(bf16[256,128]{1,0:T(8,128)(2,1)S(1)} %get-tuple-element.17.d0), channel_id=1, source_target_pairs={{0,3},{1,2},{2,1},{3,0},{4,7},{5,6},{6,5},{7,4},{8,11},{9,10},{10,... | collective-permute-start | bytes 196616 | tf_op jit(solution)/shard_map/ppermute | solution.py:512
  27.2 0.0 collective-permute-start.4
  27.2 2.5 %collective-permute-start.3 = (bf16[256,128]{1,0:T(8,128)(2,1)S(1)}, bf16[256,128]{1,0:T(8,128)(2,1)S(1)}, u32[]{:S(2)}, u32[]{:S(2)}) collective-permute-start(bf16[256,128]{1,0:T(8,128)(2,1)S(1)} %get-tuple-element.17.d0), channel_id=1, source_target_pairs={{0,1},{1,0},{2,3},{3,2},{4,5},{5,4},{6,7},{7,6},{8,9},{9,8},{10,11... | collective-permute-start | bytes 196616 | tf_op jit(solution)/shard_map/ppermute | solution.py:512
  29.7 2.3 %collective-permute-done.5.d3 = bf16[256,128]{1,0:T(8,128)(2,1)S(1)} collective-permute-done((bf16[256,128]{1,0:T(8,128)(2,1)S(1)}, bf16[256,128]{1,0:T(8,128)(2,1)S(1)}, u32[]{:S(2)}, u32[]{:S(2)}) %collective-permute-start.5) | collective-permute-done | bytes 65568 | tf_op jit(solution)/shard_map/ppermute | solution.py:512
  32.0 1.9 %collective-permute-done.4.d2 = bf16[256,128]{1,0:T(8,128)(2,1)S(1)} collective-permute-done((bf16[256,128]{1,0:T(8,128)(2,1)S(1)}, bf16[256,128]{1,0:T(8,128)(2,1)S(1)}, u32[]{:S(2)}, u32[]{:S(2)}) %collective-permute-start.4) | collective-permute-done | bytes 65568 | tf_op jit(solution)/shard_map/ppermute | solution.py:512
  33.9 0.0 collective-permute-done.3.d1
  33.9 2.2 %all-to-all-done = bf16[16,128,128]{2,1,0:T(8,128)(2,1)S(1)} async-done(((bf16[16,128,128]{2,1,0:T(8,128)(2,1)}), bf16[16,128,128]{2,1,0:T(8,128)(2,1)S(1)}, u32[]{:S(2)}, u32[]{:S(2)}) %all-to-all-start) | async-done | bytes 524320 | tf_op jit(solution)/shard_map/all_to_all | solution.py:524
  36.1 0.0 copy-done.5
  36.1 0.0 copy-done.6
  36.1 0.0 copy-done.7
  36.1 0.0 copy-done.8
  36.1 3.7 %scores_forward.1 = (bf16[1024,128]{1,0:T(8,128)(2,1)S(1)}, f32[16,2048]{1,0:T(8,128)S(1)}, f32[16,128]{1,0:T(8,128)S(1)}, f32[16,8,128]{2,1,0:T(8,128)S(1)}) custom-call(s32[4,256]{1,0:T(4,128)S(1)} %copy-done.5, s32[4,256]{1,0:T(4,128)S(1)} %copy-done.6, s32[4,256]{1,0:T(4,128)S(1)} %copy-done.7, f32[2]{0:T(128)S(1)} %copy-done.8, ...), custom_call_target="tpu_custom_call" | custom-call | tf_op jit(solution)/shard_map/scores_forward/pallas_call | solution.py:331
  39.8 11.1 %all_to_all.15.stats_ref = f32[16,8,128]{2,1,0:T(8,128)S(1)} all-to-all(f32[16,8,128]{2,1,0:T(8,128)S(1)} %get-tuple-element.21), channel_id=1, replica_groups=mesh['h'=2,'k'=2,'x'=4,'y'=4,'z'=4] {'x','y'}, dimensions={0} | all-to-all | bytes 131072 | tf_op jit(solution)/shard_map/all_to_all | solution.py:524
  50.9 0.0 copy-start.1
  50.9 0.0 copy-start.4
  50.9 5.7 %slopes.1 = (bf16[2048,128]{1,0:T(8,128)(2,1)}, f32[256,128]{1,0:T(8,128)S(1)}, f32[256,128]{1,0:T(8,128)}, f32[256,128]{1,0:T(8,128)}, f32[256,128]{1,0:T(8,128)}, /*index=5*/f32[1,128]{1,0:T(1,128)S(1)}) custom-call(s32[4,256]{1,0:T(4,128)S(1)} %copy-done.5, s32[4,256]{1,0:T(4,128)S(1)} %copy-done.6, s32[4,256]{1,0:T(4,128)S(1)} %copy-done.7, ...), custom_call_target="tpu_custom_call" | custom-call | tf_op jit(solution)/shard_map/slopes/pallas_call | solution.py:429
  56.6 4.8 %all-to-all-start.2 = ((bf16[16,128,128]{2,1,0:T(8,128)(2,1)}), bf16[16,128,128]{2,1,0:T(8,128)(2,1)S(1)}, u32[]{:S(2)}, u32[]{:S(2)}) async-start(bf16[16,128,128]{2,1,0:T(8,128)(2,1)} %bitcast.12), calls=%async_computation.2 | async-start | bytes 1048576 | tf_op jit(solution)/shard_map/all_to_all | solution.py:524
  61.4 0.1 collective-permute-start.6
  61.5 2.4 %collective-permute-start.7 = (f32[256,128]{1,0:T(8,128)}, f32[256,128]{1,0:T(8,128)}, u32[]{:S(2)}, u32[]{:S(2)}) collective-permute-start(f32[256,128]{1,0:T(8,128)} %get-tuple-element.25), channel_id=1, source_target_pairs={{0,2},{1,3},{2,0},{3,1},{4,6},{5,7},{6,4},{7,5},{8,10},{9,11},{10,... | collective-permute-start | bytes 393224 | tf_op jit(solution)/shard_map/ppermute | solution.py:512
  63.9 1.9 %collective-permute-start.8 = (f32[256,128]{1,0:T(8,128)}, f32[256,128]{1,0:T(8,128)}, u32[]{:S(2)}, u32[]{:S(2)}) collective-permute-start(f32[256,128]{1,0:T(8,128)} %get-tuple-element.26), channel_id=1, source_target_pairs={{0,3},{1,2},{2,1},{3,0},{4,7},{5,6},{6,5},{7,4},{8,11},{9,10},{10,... | collective-permute-start | bytes 393224 | tf_op jit(solution)/shard_map/ppermute | solution.py:512
  65.8 0.6 constant_dynamic-slice_fusion
  66.4 1.1 %collective-permute-done.6.g1 = f32[256,128]{1,0:T(8,128)} collective-permute-done((f32[256,128]{1,0:T(8,128)}, f32[256,128]{1,0:T(8,128)}, u32[]{:S(2)}, u32[]{:S(2)}) %collective-permute-start.6) | collective-permute-done | bytes 131104 | tf_op jit(solution)/shard_map/ppermute | solution.py:512
  67.5 6.0 %collective-permute-done.7.g2 = f32[256,128]{1,0:T(8,128)} collective-permute-done((f32[256,128]{1,0:T(8,128)}, f32[256,128]{1,0:T(8,128)}, u32[]{:S(2)}, u32[]{:S(2)}) %collective-permute-start.7) | collective-permute-done | bytes 131104 | tf_op jit(solution)/shard_map/ppermute | solution.py:512
  73.5 0.0 collective-permute-done.8.g3
  73.5 0.0 all-to-all-done.2.gq_ref
  73.5 0.0 copy-done.1
  73.5 0.0 copy-done.4
  73.5 3.4 %head_backward.1 = bf16[4,96,2048]{2,1,0:T(8,128)(2,1)} custom-call(bf16[4,96,2048]{2,1,0:T(8,128)(2,1)S(1)} %bitcast.6, f32[1,2048]{1,0:T(1,128)S(1)} %bitcast.10, bf16[2048,128]{1,0:T(8,128)(2,1)S(1)} %assemble.1.emb_ref, f32[4,96,128]{2,1,0:T(8,128)S(1)} %get-tuple-element.15.proj_ref, bf16[16,128,128]{2,1,0:T(8,128)(2,1)S(1)} %all-to-all-done.2.gq_ref, ...), custom_call_target="tpu_custom_call" | custom-call | tf_op jit(solution)/shard_map/head_backward/pallas_call | solution.py:488
  (1 shorter events, 0.0 us)
Async XLA Ops:
  0.6 12.5 %collective-permute-start.1 = (bf16[512,128]{1,0:T(8,128)(2,1)}, bf16[512,128]{1,0:T(8,128)(2,1)S(1)}, u32[]{:S(2)}, u32[]{:S(2)}) collective-permute-start(bf16[512,128]{1,0:T(8,128)(2,1)} %own_ref.3), channel_id=1, source_target_pairs={{0,131},{1,130},{2,129},{3,128},{128,3},{129,2},{130,1},{131,0},{4... | collective-permute-start | bytes 393224 | tf_op jit(solution)/shard_map/ppermute | solution.py:505
  6.6 9.4 %collective-permute-start = (bf16[512,128]{1,0:T(8,128)(2,1)}, bf16[512,128]{1,0:T(8,128)(2,1)S(1)}, u32[]{:S(2)}, u32[]{:S(2)}) collective-permute-start(bf16[512,128]{1,0:T(8,128)(2,1)} %own_ref.3), channel_id=1, source_target_pairs={{0,64},{64,0},{1,65},{65,1},{2,66},{66,2},{3,67},{67,3},{4,68},{68... | collective-permute-start | bytes 393224 | tf_op jit(solution)/shard_map/ppermute | solution.py:506
  13.1 3.5 %collective-permute-start.2 = (bf16[512,128]{1,0:T(8,128)(2,1)S(1)}, bf16[512,128]{1,0:T(8,128)(2,1)S(1)}, u32[]{:S(2)}, u32[]{:S(2)}) collective-permute-start(bf16[512,128]{1,0:T(8,128)(2,1)S(1)} %collective-permute-done.1.far_ref), channel_id=1, source_target_pairs={{0,64},{64,0},{1,65},{65,1},{2,66},{66,2},{3,67},{67,3},{4,68},{68... | collective-permute-start | bytes 393224 | tf_op jit(solution)/shard_map/ppermute | solution.py:507
  13.1 1.4 %copy-start = (bf16[1,4,96,2048]{3,2,1,0:T(8,128)(2,1)S(1)}, bf16[1,4,96,2048]{3,2,1,0:T(8,128)(2,1)}, u32[]{:S(2)}) copy-start(bf16[1,4,96,2048]{3,2,1,0:T(8,128)(2,1)} %param.7) | copy-start | bytes 4718596
  14.5 0.7 copy-start.3
  15.2 0.9 %copy-start.2 = (bf16[512,128]{1,0:T(8,128)(2,1)S(1)}, bf16[512,128]{1,0:T(8,128)(2,1)}, u32[]{:S(2)}) copy-start(bf16[512,128]{1,0:T(8,128)(2,1)} %own_ref.3) | copy-start | bytes 393220
  16.6 19.5 %copy-start.5 = (s32[4,256]{1,0:T(4,128)S(1)}, s32[4,256]{1,0:T(4,128)}, u32[]{:S(2)}) copy-start(s32[4,256]{1,0:T(4,128)} %request_ref.3) | copy-start | bytes 12292
  16.6 19.5 %copy-start.6 = (s32[4,256]{1,0:T(4,128)S(1)}, s32[4,256]{1,0:T(4,128)}, u32[]{:S(2)}) copy-start(s32[4,256]{1,0:T(4,128)} %passage_ref.3) | copy-start | bytes 12292
  16.6 19.5 %copy-start.7 = (s32[4,256]{1,0:T(4,128)S(1)}, s32[4,256]{1,0:T(4,128)}, u32[]{:S(2)}) copy-start(s32[4,256]{1,0:T(4,128)} %match_ref.3) | copy-start | bytes 12292
  16.6 19.5 %copy-start.8 = (f32[2]{0:T(128)S(1)}, f32[2]{0:T(128)}, u32[]{:S(2)}) copy-start(f32[2]{0:T(128)} %steep_ref.3) | copy-start | bytes 28
  17.9 18.2 %all-to-all-start = ((bf16[16,128,128]{2,1,0:T(8,128)(2,1)}), bf16[16,128,128]{2,1,0:T(8,128)(2,1)S(1)}, u32[]{:S(2)}, u32[]{:S(2)}) async-start(bf16[16,128,128]{2,1,0:T(8,128)(2,1)} %get-tuple-element.16), calls=%async_computation | async-start | bytes 1048576 | tf_op jit(solution)/shard_map/all_to_all | solution.py:524
  25.3 6.7 %collective-permute-start.5 = (bf16[256,128]{1,0:T(8,128)(2,1)S(1)}, bf16[256,128]{1,0:T(8,128)(2,1)S(1)}, u32[]{:S(2)}, u32[]{:S(2)}) collective-permute-start(bf16[256,128]{1,0:T(8,128)(2,1)S(1)} %get-tuple-element.17.d0), channel_id=1, source_target_pairs={{0,3},{1,2},{2,1},{3,0},{4,7},{5,6},{6,5},{7,4},{8,11},{9,10},{10,... | collective-permute-start | bytes 196616 | tf_op jit(solution)/shard_map/ppermute | solution.py:512
  27.2 6.7 %collective-permute-start.4 = (bf16[256,128]{1,0:T(8,128)(2,1)S(1)}, bf16[256,128]{1,0:T(8,128)(2,1)S(1)}, u32[]{:S(2)}, u32[]{:S(2)}) collective-permute-start(bf16[256,128]{1,0:T(8,128)(2,1)S(1)} %get-tuple-element.17.d0), channel_id=1, source_target_pairs={{0,2},{1,3},{2,0},{3,1},{4,6},{5,7},{6,4},{7,5},{8,10},{9,11},{10,... | collective-permute-start | bytes 196616 | tf_op jit(solution)/shard_map/ppermute | solution.py:512
  27.2 6.7 %collective-permute-start.3 = (bf16[256,128]{1,0:T(8,128)(2,1)S(1)}, bf16[256,128]{1,0:T(8,128)(2,1)S(1)}, u32[]{:S(2)}, u32[]{:S(2)}) collective-permute-start(bf16[256,128]{1,0:T(8,128)(2,1)S(1)} %get-tuple-element.17.d0), channel_id=1, source_target_pairs={{0,1},{1,0},{2,3},{3,2},{4,5},{5,4},{6,7},{7,6},{8,9},{9,8},{10,11... | collective-permute-start | bytes 196616 | tf_op jit(solution)/shard_map/ppermute | solution.py:512
  50.9 22.6 %copy-start.1 = (bf16[1,4,96,2048]{3,2,1,0:T(8,128)(2,1)S(1)}, bf16[1,4,96,2048]{3,2,1,0:T(8,128)(2,1)}, u32[]{:S(2)}) copy-start(bf16[1,4,96,2048]{3,2,1,0:T(8,128)(2,1)} %param.7) | copy-start | bytes 4718596
  50.9 22.6 %copy-start.4 = (f32[2048]{0:T(1024)S(1)}, f32[2048]{0:T(1024)}, u32[]{:S(2)}) copy-start(f32[2048]{0:T(1024)} %param.8) | copy-start | bytes 24580
  56.6 17.0 %all-to-all-start.2 = ((bf16[16,128,128]{2,1,0:T(8,128)(2,1)}), bf16[16,128,128]{2,1,0:T(8,128)(2,1)S(1)}, u32[]{:S(2)}, u32[]{:S(2)}) async-start(bf16[16,128,128]{2,1,0:T(8,128)(2,1)} %bitcast.12), calls=%async_computation.2 | async-start | bytes 1048576 | tf_op jit(solution)/shard_map/all_to_all | solution.py:524
  61.4 6.1 %collective-permute-start.6 = (f32[256,128]{1,0:T(8,128)}, f32[256,128]{1,0:T(8,128)}, u32[]{:S(2)}, u32[]{:S(2)}) collective-permute-start(f32[256,128]{1,0:T(8,128)} %get-tuple-element.24), channel_id=1, source_target_pairs={{0,1},{1,0},{2,3},{3,2},{4,5},{5,4},{6,7},{7,6},{8,9},{9,8},{10,11... | collective-permute-start | bytes 393224 | tf_op jit(solution)/shard_map/ppermute | solution.py:512
  61.5 12.0 %collective-permute-start.7 = (f32[256,128]{1,0:T(8,128)}, f32[256,128]{1,0:T(8,128)}, u32[]{:S(2)}, u32[]{:S(2)}) collective-permute-start(f32[256,128]{1,0:T(8,128)} %get-tuple-element.25), channel_id=1, source_target_pairs={{0,2},{1,3},{2,0},{3,1},{4,6},{5,7},{6,4},{7,5},{8,10},{9,11},{10,... | collective-permute-start | bytes 393224 | tf_op jit(solution)/shard_map/ppermute | solution.py:512
  63.9 9.7 %collective-permute-start.8 = (f32[256,128]{1,0:T(8,128)}, f32[256,128]{1,0:T(8,128)}, u32[]{:S(2)}, u32[]{:S(2)}) collective-permute-start(f32[256,128]{1,0:T(8,128)} %get-tuple-element.26), channel_id=1, source_target_pairs={{0,3},{1,2},{2,1},{3,0},{4,7},{5,6},{6,5},{7,4},{8,11},{9,10},{10,... | collective-permute-start | bytes 393224 | tf_op jit(solution)/shard_map/ppermute | solution.py:512
